TPU v7x, 128 devices: a whole 4x4x4 slice. The times are simulated.
128 devices in a mesh: front: 4 (over x_lo, core), row: 4 (over z), col: 8 (over y, x_hi).
Axes of the slice: x: 4 (x_hi: 2, x_lo: 2; x = x_hi * 2 + x_lo), y: 4, z: 4, core: 2. Of those that a mesh axis runs over, the one named last changes fastest.
Arguments:
- front_entries: float32 [4, 8192, 8192], P('front', 'row', 'col'), may hold values from -12 to 128, as said below
- kid_u: bfloat16 [16, 4096, 128], P('front', ('row', 'col')), may hold values from -0.7109375 to 0.7109375
- kid_v: bfloat16 [16, 4096, 128], P('front', ('row', 'col')), may hold values from -0.7109375 to 0.7109375
- kid_d: bfloat16 [16, 4096, 256], P('front', ('row', 'col')), may hold values from -2.09375 to 2.09375
- kid_counts: int32 [16], replicated, may hold values from 32 to 128
- kid_blocks: int32 [16, 16], replicated, may hold values from 0 to 31, as said below
Outputs:
- front_out: float32 [4, 8192, 8192], P('front', 'row', 'col')
Inputs may be any that keep to these rules, and one draw needn't show every extreme that they name: `front_entries`: diagonal entries lie between 64 and 128; the other entries are of order one. `kid_blocks`: each row holds distinct block positions in increasing order. `kid_counts`: rank columns at or beyond a child's count are padding.
All inputs are finite; a program needn't handle non-finite values.
Results may differ from a plain program's by a relative error of at most 0.004.
Values may be sent and summed in bfloat16 or wider, within the bound.
No kernel may reach another device: no remote copies, remote signals or barrier semaphores. Data moves between devices by JAX's collectives and lax.ppermute only.
A program may use at most 128 MiB of HBM per device.

v0:
```python
import jax
import jax.numpy as jnp
from jax import lax
from jax.experimental import pallas as pl
from jax.experimental.pallas import tpu as pltpu
from jax.sharding import Mesh
from jax.sharding import PartitionSpec as P


PANEL = 256
PANELS = 4
K = PANEL * PANELS
COL = ("col_0", "col_1")
ROW_COL = ("row", "col_0", "col_1")
F32 = jnp.float32
BF16 = jnp.bfloat16


def dot(a, b):
    return jnp.dot(a, b, preferred_element_type=F32)


def split(a):
    high = a.astype(BF16)
    return high, (a - high.astype(F32)).astype(BF16)


def total(flags, values):
    out = None
    for flag, value in zip(flags, values):
        piece = jnp.where(flag, value, jnp.zeros_like(value))
        out = piece if out is None else out + piece
    return out


SHIFT = 96.0


def identity():
    rows = lax.broadcasted_iota(jnp.int32, (PANEL, PANEL), 0)
    return rows == lax.broadcasted_iota(jnp.int32, (PANEL, PANEL), 1)


def invert_into(inv, index, pivot):
    eye = identity()
    one = jnp.where(eye, 1.0, 0.0)
    diagonal = jnp.where(eye, pivot, 0.0)
    down = 1.0 / jnp.sum(diagonal, axis=1, keepdims=True)
    across = 1.0 / jnp.sum(diagonal, axis=0, keepdims=True)
    rest = jnp.where(eye, 0.0, -pivot * across)
    power = rest.astype(BF16)
    series = one + rest
    for _ in range(3):
        power = dot(power, power).astype(BF16)
        series = series + dot(series.astype(BF16), power)
    inv[index] = series * down
    p_high, p_low = split(pivot)

    def improve():
        x = inv[index]
        x_high, x_low = split(x)
        error = one - (dot(p_high, x_high) + (dot(p_high, x_low) + dot(p_low, x_high)))
        inv[index] = x + dot(x_high, error.astype(BF16))
        square = error * error
        return jnp.max(jnp.sum(square, axis=0)) * jnp.max(jnp.sum(square, axis=1))

    size = improve()

    @pl.when(jnp.logical_not(size < 0.5))
    def _():
        norm = jnp.max(jnp.sum(jnp.abs(pivot), axis=0)) * jnp.max(jnp.sum(jnp.abs(pivot), axis=1))
        inv[index] = pivot.T * (1.0 / norm)

    def more(carry):
        trips, _ = carry
        return trips + 1, improve()

    lax.while_loop(
        lambda carry: (carry[0] < 100) & jnp.logical_not(carry[1] < 4e-6), more, (jnp.int32(0), size)
    )


def factor_kernel(scal, tile, top, kc, g0, g1, g2, g3, a, c, inv):
    outs = (g0, g1, g2, g3)
    row, place = scal[0], scal[3]

    @pl.when(row == 0)
    def _():
        a[...] = top[...].astype(F32)
        for k in range(PANELS):
            s, e = k * PANEL, (k + 1) * PANEL
            a[s:e, s:e] = a[s:e, s:e] + jnp.where(identity(), SHIFT, 0.0)

        @pl.when(place == 0)
        def _():
            c[...] = a[...]

        @pl.when(place != 0)
        def _():
            c[...] = tile[...]

        for k in range(PANELS):
            s, e = k * PANEL, (k + 1) * PANEL
            invert_into(inv, k, a[s:e, s:e])
            if e < K:
                lower = dot(a[e:, s:e].astype(BF16), inv[k].astype(BF16))
                a[e:, s:e] = lower
                lower_b = lower.astype(BF16)
                a[e:, e:] = a[e:, e:] - dot(lower_b, a[s:e, e:].astype(BF16))
                c[e:, :] = c[e:, :] - dot(lower_b, c[s:e, :].astype(BF16))

        @pl.when(place == 0)
        def _():
            kc[...] = a[...]
            rows = lax.broadcasted_iota(jnp.int32, (K, K), 0)
            cols = lax.broadcasted_iota(jnp.int32, (K, K), 1)
            c[...] = jnp.where(rows == cols, 1.0, 0.0)

        @pl.when(place != 0)
        def _():
            kc[...] = c[...]

        for k in reversed(range(PANELS)):
            s, e = k * PANEL, (k + 1) * PANEL
            part = dot(inv[k].astype(BF16), c[s:e, :].astype(BF16))
            part_b = part.astype(BF16)
            for q in range(4):
                outs[q][s:e, :] = part_b[:, q * PANEL : (q + 1) * PANEL]
            if k:
                c[:s, :] = c[:s, :] - dot(a[:s, s:e].astype(BF16), part_b)


def whole(shape):
    return pl.BlockSpec(shape, lambda i, s: (0,) * len(shape))


def call(kernel, scal, args, in_specs, outs, out_specs, grid=(1,), scratch=(), flops=0):
    moved = sum(x.size * x.dtype.itemsize for x in args)
    single = not isinstance(outs, tuple)
    return pl.pallas_call(
        kernel,
        out_shape=outs,
        grid_spec=pltpu.PrefetchScalarGridSpec(
            num_scalar_prefetch=1,
            grid=grid,
            in_specs=in_specs,
            out_specs=out_specs if single else tuple(out_specs),
            scratch_shapes=list(scratch),
        ),
        compiler_params=pltpu.CompilerParams(vmem_limit_bytes=56 * 1024 * 1024),
        cost_estimate=pl.CostEstimate(flops=flops, bytes_accessed=2 * moved, transcendentals=0),
    )(scal, *args)


def simple(kernel, scal, args, outs, scratch=(), flops=0):
    return call(
        kernel, scal, args, [whole(x.shape) for x in args], tuple(outs),
        [whole(x.shape) for x in outs], scratch=scratch, flops=flops,
    )


def shape(*dims, dtype=BF16):
    return jax.ShapeDtypeStruct(dims, dtype)


def factor(scal, tile, top):
    return call(
        factor_kernel, scal, [tile, top],
        [whole((K, K)), whole((K, K))],
        (shape(K, K, dtype=F32),) + (shape(K, PANEL),) * 4,
        [whole((K, K))] + [whole((K, PANEL))] * 4,
        scratch=[pltpu.VMEM((K, K), F32), pltpu.VMEM((K, K), F32), pltpu.VMEM((PANELS, PANEL, PANEL), F32)],
        flops=10 * K * K * K,
    )


COUNT_AT, BLOCK_AT = 4, 8


def block_of(scal, kid, source_row, q):
    return scal[BLOCK_AT + kid * 16 + source_row * 4 + q]


def spot(scal, kid, window, q):
    at = jnp.int32(-1)
    for source_row in range(4):
        block = block_of(scal, kid, source_row, q)
        at = jnp.where((block >> 2) == window, block & 3, at)
    return at


def chosen(flags, values):
    acc = None
    for flag, value in zip(flags, values):
        value = value.astype(F32)
        value = jnp.where(flag, value, jnp.zeros_like(value))
        acc = value if acc is None else acc + value
    return acc


def halve_kernel(scal, front, *outs):
    for i, out in enumerate(outs):
        out[...] = front[i * PANEL : (i + 1) * PANEL, :].astype(BF16)


def halve(scal, front, part):
    return call(
        halve_kernel, scal, [front], [pl.BlockSpec((K, K), lambda i, s: (part, 0))],
        (shape(PANEL, K),) * 4, [whole((PANEL, K))] * 4,
    )


def pick_left_kernel(scal, u0, u1, u2, u3, out):
    row, y = scal[0], scal[1]
    lane = lax.broadcasted_iota(jnp.int32, (128, 128), 1)
    for kid in range(4):
        live = lane < scal[COUNT_AT + kid]
        blocks = [block_of(scal, kid, (row - k) & 3, y) for k in range(4)]
        for window in range(2):
            flags = [(b >> 2) == 2 * row + window for b in blocks]
            value = chosen(flags, [u[kid] for u in (u0, u1, u2, u3)])
            value = jnp.where(live, value, 0.0).astype(BF16)
            for peer in range(8):
                out[peer, window, kid] = value


def pick_right_kernel(scal, p0, p1, p2, p3, out):
    row, y = scal[0], scal[1]
    blocks = [block_of(scal, row, (row - k) & 3, y) for k in range(4)]
    rights = [p[...] for p in (p0, p1, p2, p3)]
    first = chosen([(b >> 2) == 0 for b in blocks], rights).astype(BF16)
    for peer in range(8):
        out[peer, :, :128] = chosen([(b >> 2) == peer for b in blocks], rights).astype(BF16)
        out[peer, :, 128:] = first


def pick_blocks_kernel(scal, d0, d1, d2, d3, out):
    row, y = scal[0], scal[1]
    for window in range(8):
        flags, values = [], []
        for kid in range(4):
            for k, d in enumerate((d0, d1, d2, d3)):
                flags.append(block_of(scal, kid, (row - k) & 3, y) == 4 * window + row)
                values.append(d[kid])
        out[window] = chosen(flags, values).astype(BF16)


def place_right_kernel(scal, back, out_own, out_first):
    row, place = scal[0], scal[3]
    own = [spot(scal, row, place, q) for q in range(4)]
    first = [spot(scal, row, 0, q) for q in range(4)]
    for at in range(4):
        for half in range(2):
            rows = slice((2 * at + half) * 128, (2 * at + half + 1) * 128)
            for spots, out, cols in ((own, out_own, slice(0, 128)), (first, out_first, slice(128, 256))):
                flags = [spots[q] == at for q in range(4)]
                out[rows, :] = chosen(flags, [back[2 * q + half, :, cols] for q in range(4)]).astype(BF16)


def place_blocks_kernel(scal, back, out):
    for half in range(2):
        acc = back[half].astype(F32)
        for q in range(1, 4):
            acc = acc + back[2 * q + half].astype(F32)
        out[half * 128 : (half + 1) * 128, :] = acc.astype(BF16)


def slab_kernel(scal, near, far, us, *refs, part):
    vs, ks = refs[:4], refs[4:-4]
    out, left, right, acc = refs[-4:]
    row, y, h, place = scal[0], scal[1], scal[2], scal[3]
    for s in range(4):
        kid = (row - s) & 3
        right[:, s * 128 : (s + 1) * 128] = vs[s][...]
        hits = [spot(scal, kid, 2 * row + part, q) == y for q in range(4)]
        value = chosen(hits, [us[2 * q + h, part, kid] for q in range(4)])
        left[:, s * 128 : (s + 1) * 128] = value.astype(BF16)
    raw = jnp.where(h == 0, near[:128, :].astype(F32), far[...].astype(F32))
    acc[...] = raw + lax.dot_general(
        left[...], right[...], (((1,), (1,)), ((), ())), preferred_element_type=F32
    )
    if ks:
        @pl.when(row == 0)
        def _():
            extra = ks[0][...].astype(F32) + ks[1][...].astype(F32)
            for at in range(4):
                @pl.when(y == at)
                def _(at=at):
                    cols = slice(at * PANEL, (at + 1) * PANEL)
                    acc[:, cols] = acc[:, cols] + extra
            rows = lax.broadcasted_iota(jnp.int32, (128, K), 0)
            cols = lax.broadcasted_iota(jnp.int32, (128, K), 1)
            acc[...] = acc[...] - jnp.where(cols == rows + place * 128, SHIFT, 0.0)

    final = acc[...].astype(BF16)
    for peer in range(8):
        out[peer] = final


def slab(scal, part, raws, us, vs, ks):
    args = list(raws) + [us] + list(vs) + list(ks)
    return simple(
        lambda *refs: slab_kernel(*refs, part=part), scal, args, [shape(8, 128, K)],
        scratch=[pltpu.VMEM((128, 512), BF16), pltpu.VMEM((K, 512), BF16), pltpu.VMEM((128, K), F32)],
        flops=2 * 128 * K * 512,
    )[0]


def assemble_kernel(scal, front, us, v0, v1, v2, v3, out, left, right):
    row = scal[0]
    step = pl.program_id(0)
    window, at = step // 4, step % 4

    @pl.when(step == 0)
    def _():
        for s, v in enumerate((v0, v1, v2, v3)):
            right[:, s * 128 : (s + 1) * 128] = v[...]

    for s in range(4):
        kid = (row - s) & 3
        hits = [spot(scal, kid, 2 * row + window, q) == at for q in range(4)]
        for half in range(2):
            value = chosen(hits, [us[2 * q + half, window, kid] for q in range(4)])
            left[half * 128 : (half + 1) * 128, s * 128 : (s + 1) * 128] = value.astype(BF16)
    out[...] = front[...] + lax.dot_general(
        left[...], right[...], (((1,), (1,)), ((), ())), preferred_element_type=F32
    )


def assemble(scal, front, us, vs):
    rows, cols = front.shape
    args = [front, us] + list(vs)
    block = pl.BlockSpec((PANEL, cols), lambda i, s: (i, 0))
    return call(
        assemble_kernel, scal, args,
        [block] + [whole(x.shape) for x in args[1:]],
        shape(rows, cols, dtype=F32), block, grid=(rows // PANEL,),
        scratch=[pltpu.VMEM((PANEL, 512), BF16), pltpu.VMEM((cols, 512), BF16)],
        flops=2 * rows * cols * 512,
    )


TALL = 2 * PANEL


def trail_kernel(scal, tile, kc, top, low, g0, g1, g2, g3, d0, d1, d2, d3, out):
    row, y, h, place = scal[0], scal[1], scal[2], scal[3]
    step = pl.program_id(0)
    gs = (g0, g1, g2, g3)

    @pl.when((row == 0) & (step < 2))
    def _():
        out[...] = kc[...]

    def update(rows):
        @pl.when(place == 0)
        def _():
            for q, g in enumerate(gs):
                out[:, q * PANEL : (q + 1) * PANEL] = dot(rows[...], g[...])

        @pl.when(place != 0)
        def _():
            for q, g in enumerate(gs):
                cols = slice(q * PANEL, (q + 1) * PANEL)
                out[:, cols] = tile[:, cols] - dot(rows[...], g[...])
            for s, d in enumerate((d0, d1, d2, d3)):
                for at in range(4):
                    @pl.when((row == y) & (step == 2 * h + at // 2) & (((row - s) & 3) == at))
                    def _(at=at, d=d):
                        rows_at = slice(at % 2 * PANEL, (at % 2 + 1) * PANEL)
                        cols = slice(at * PANEL, (at + 1) * PANEL)
                        out[rows_at, cols] = out[rows_at, cols] + d[...].astype(F32)

    @pl.when((row != 0) & (step < 2))
    def _():
        update(top)

    @pl.when(step >= 2)
    def _():
        update(low)


def trail(scal, tile, kc, top, low, gs, ds):
    rows, cols = tile.shape
    block = pl.BlockSpec((TALL, cols), lambda i, s: (i, 0))
    first = pl.BlockSpec((TALL, cols), lambda i, s: (jnp.minimum(i, 1), 0))
    second = pl.BlockSpec((TALL, cols), lambda i, s: (jnp.maximum(i, 2) - 2, 0))
    args = [tile, kc, top, low] + list(gs) + list(ds)
    return call(
        trail_kernel, scal, args,
        [block, first, first, second] + [whole(x.shape) for x in args[4:]],
        shape(rows, cols, dtype=F32), block, grid=(rows // TALL,),
        flops=2 * rows * cols * K,
    )


def spread(pieces, y):
    got = [pieces[0]] + [lax.ppermute(pieces[i], COL, [(0, 2 * i)]) for i in range(1, 4)]
    mine = total([y == i for i in range(4)], got)
    return mine, lax.ppermute(mine[128:], COL, [(2 * i, 2 * i + 1) for i in range(4)])


def over_rows(value):
    return [value] + [
        lax.ppermute(value, "row", [(i, (i + s) % 4) for i in range(4)]) for s in range(1, 4)
    ]


def after(value, token):
    return lax.optimization_barrier((value, token))[0]


def local(front_entries, kid_u, kid_v, kid_d, kid_counts, kid_blocks):
    children, _, rank = kid_u.shape
    f = lax.axis_index("front")
    r = lax.axis_index("row")
    y = lax.axis_index("col_0")
    h = lax.axis_index("col_1")
    place = 2 * y + h
    first_child = (f + 3) % 4 * children
    counts = lax.dynamic_slice_in_dim(kid_counts, first_child, children, 0)
    blocks = lax.dynamic_slice_in_dim(kid_blocks, first_child, children, 0)
    scal = jnp.concatenate((jnp.stack([r, y, h, place]), counts, blocks.reshape(-1))).astype(jnp.int32)
    front = front_entries[0]

    def moved(make):
        out = []
        for k in range(4):
            pairs = [(i * 4 + j, (i + 1) % 4 * 4 + (j + k) % 4) for i in range(4) for j in range(4)]
            out.append(lax.ppermute(make(k), ("front", "row"), pairs))
        return out

    got_p = moved(lambda k: lax.dynamic_index_in_dim(kid_v, (r + k) % 4, 0, keepdims=False))
    got_u = moved(lambda k: kid_u)
    got_d = moved(lambda k: kid_d)

    send = simple(pick_right_kernel, scal, got_p, [shape(8, 128, 256)])[0]
    back_v = lax.all_to_all(send, COL, 0, 0)
    slots = simple(pick_left_kernel, scal, got_u, [shape(8, 2, 4, 128, rank)])[0]
    all_u = lax.all_to_all(after(slots, back_v[0, 0, 0]), COL, 0, 0)
    raw_top = spread(halve(scal, front, 0), y)
    raw_low = spread(halve(scal, front, 1), y)
    send = simple(pick_blocks_kernel, scal, got_d, [shape(8, 128, PANEL)])[0]
    back_d = lax.all_to_all(after(send, all_u[0, 0, 0, 0, 0]), COL, 0, 0)
    v_own, v_first = simple(place_right_kernel, scal, [back_v], [shape(K, rank), shape(K, rank)])
    vs_first = over_rows(v_first)
    d_mine = simple(place_blocks_kernel, scal, [back_d], [shape(PANEL, PANEL)])[0]
    ks = [
        lax.ppermute(d_mine[half * 128 : (half + 1) * 128], ROW_COL, [(8 * p, 2 * p + half) for p in range(4)])
        for half in range(2)
    ]
    slab_top = slab(scal, 0, raw_top, all_u, vs_first, ks)
    top = lax.all_to_all(slab_top, COL, 0, 0).reshape(K, K)
    token = slab_top[0, 0, 0]
    slab_low = slab(scal, 1, raw_low, all_u, vs_first, ())
    vs = over_rows(after(v_own, token))
    ds = [d_mine]
    for s in range(1, 4):
        pairs = [
            (((t - s) % 4) * 8 + 2 * t + x, t * 8 + 2 * t + x) for t in range(4) for x in range(2)
        ]
        ds.append(lax.ppermute(after(d_mine, token), ROW_COL, pairs))
    tile = assemble(scal, front, all_u, vs)
    kc, *g = factor(scal, tile, top)
    low = lax.all_to_all(after(slab_low, kc[0, 0]), COL, 0, 0).reshape(K, K)

    def up(value, hops):
        return lax.ppermute(value, "row", [(i, i + 1) for i in range(hops)])

    def down(value, hops):
        return lax.ppermute(value, "row", [(-i % 4, -(i + 1) % 4) for i in range(hops)])

    root = r == 0
    up1, down1 = lax.optimization_barrier((up(g[0], 1), down(g[3], 1)))
    pair = lax.optimization_barrier((jnp.where(root, g[1], up1), jnp.where(root, g[2], down1)))
    up2, down2 = lax.optimization_barrier((up(pair[0], 2), down(pair[1], 2)))
    pair = lax.optimization_barrier((jnp.where(root, g[2], up2), jnp.where(root, g[1], down2)))
    up3, down3 = up(pair[0], 3), down(pair[1], 3)
    rows_are = [r == i for i in range(4)]
    quarters = [
        total(rows_are, (g[0], up1, up2, up3)),
        total(rows_are, (g[1], up2, up3, down3)),
        total(rows_are, (g[2], up3, down3, down2)),
        total(rows_are, (g[3], down3, down2, down1)),
    ]
    return trail(scal, tile, kc, top, low, quarters, ds)[None]


def solution(mesh):
    finer = Mesh(
        mesh.devices.reshape(mesh.shape["front"], mesh.shape["row"], 4, 2),
        ("front", "row", "col_0", "col_1"),
    )
    in_specs = (
        P("front", "row", COL),
        P("front", ROW_COL, None),
        P("front", ROW_COL, None),
        P("front", ROW_COL, None),
        P(),
        P(),
    )
    out_specs = P("front", "row", COL)
    return jax.shard_map(local, mesh=finer, in_specs=in_specs, out_specs=out_specs, check_vma=False)
```

profile of v0, /device:TPU:2, one launch (start us, length us, event | category | flops | bytes accessed | tf_op | source)
XLA Modules:
  0.0 266.6 jit_solution(14214038010854403128)
XLA Ops:
  0.9 3.5 %collective-permute-start.7 = (bf16[128,128]{1,0:T(8,128)(2,1)S(1)}, bf16[128,128]{1,0:T(8,128)(2,1)S(1)}, u32[]{:S(2)}, u32[]{:S(2)}) collective-permute-start(bf16[128,128]{1,0:T(8,128)(2,1)S(1)} %get-tuple-element.61), channel_id=1, source_target_pairs={{0,56},{8,32},{16,40},{24,48},{32,88},{40,64},{48,72},{56,80},{64,... | collective-permute-start | bytes 98312 | tf_op jit(solution)/shard_map/ppermute | solution.py:430
  13.9 6.3 %all-to-all-start.1 = ((bf16[8,128,256]{2,1,0:T(8,128)(2,1)}), bf16[8,128,256]{2,1,0:T(8,128)(2,1)S(1)}, u32[]{:S(2)}, u32[]{:S(2)}) async-start(bf16[8,128,256]{2,1,0:T(8,128)(2,1)} %shard_map.65), calls=%async_computation.1 | async-start | bytes 1048576 | tf_op jit(solution)/shard_map/all_to_all | solution.py:438
  25.6 9.2 %collective-permute-done.16.d1 = bf16[4,128,256]{2,1,0:T(8,128)(2,1)S(1)} collective-permute-done((bf16[4,128,256]{2,1,0:T(8,128)(2,1)S(1)}, bf16[4,128,256]{2,1,0:T(8,128)(2,1)S(1)}, u32[]{:S(2)}, u32[]{:S(2)}) %collective-permute-start.16) | collective-permute-done | bytes 262176 | tf_op jit(solution)/shard_map/ppermute | solution.py:430
  36.7 4.2 %collective-permute-done.17.d2 = bf16[4,128,256]{2,1,0:T(8,128)(2,1)S(1)} collective-permute-done((bf16[4,128,256]{2,1,0:T(8,128)(2,1)S(1)}, bf16[4,128,256]{2,1,0:T(8,128)(2,1)S(1)}, u32[]{:S(2)}, u32[]{:S(2)}) %collective-permute-start.17) | collective-permute-done | bytes 262176 | tf_op jit(solution)/shard_map/ppermute | solution.py:430
  41.5 4.3 %shard_map.68 = bf16[8,128,256]{2,1,0:T(8,128)(2,1)} custom-call(s32[72]{0:T(128)} %concatenate.3.scal.refs_0_, bf16[4,128,256]{2,1,0:T(8,128)(2,1)} %copy-done.26, bf16[4,128,256]{2,1,0:T(8,128)(2,1)} %copy-done.25, bf16[4,128,256]{2,1,0:T(8,128)(2,1)} %copy-done.28, bf16[4,128,256]{2,1,0:T(8,128)(2,1)} %copy-done.27), custom_call_target="tpu_custom_call" | custom-call | bytes 2097152 | tf_op jit(solution)/shard_map/pallas_call | solution.py:140
  45.9 6.3 %all-to-all-start.2 = ((bf16[8,128,256]{2,1,0:T(8,128)(2,1)}), bf16[8,128,256]{2,1,0:T(8,128)(2,1)S(1)}, u32[]{:S(2)}, u32[]{:S(2)}) async-start(bf16[8,128,256]{2,1,0:T(8,128)(2,1)} %shard_map.68), calls=%async_computation.2 | async-start | bytes 1048576 | tf_op jit(solution)/shard_map/all_to_all | solution.py:444
  52.3 3.6 %collective-permute-start = (bf16[4,128,128]{2,1,0:T(8,128)(2,1)S(1)}, bf16[4,128,128]{2,1,0:T(8,128)(2,1)S(1)}, u32[]{:S(2)}, u32[]{:S(2)}) collective-permute-start(bf16[4,128,128]{2,1,0:T(8,128)(2,1)S(1)} %copy-done.42), channel_id=1, source_target_pairs={{0,32},{8,40},{16,48},{24,56},{32,64},{40,72},{48,80},{56,88},{64,... | collective-permute-start | bytes 393224 | tf_op jit(solution)/shard_map/ppermute | solution.py:430
  57.7 3.5 %collective-permute-done.1.u1 = bf16[4,128,128]{2,1,0:T(8,128)(2,1)S(1)} collective-permute-done((bf16[4,128,128]{2,1,0:T(8,128)(2,1)S(1)}, bf16[4,128,128]{2,1,0:T(8,128)(2,1)S(1)}, u32[]{:S(2)}, u32[]{:S(2)}) %collective-permute-start.1) | collective-permute-done | bytes 131104 | tf_op jit(solution)/shard_map/ppermute | solution.py:430
  62.5 3.0 %collective-permute-done.2.u2 = bf16[4,128,128]{2,1,0:T(8,128)(2,1)S(1)} collective-permute-done((bf16[4,128,128]{2,1,0:T(8,128)(2,1)S(1)}, bf16[4,128,128]{2,1,0:T(8,128)(2,1)S(1)}, u32[]{:S(2)}, u32[]{:S(2)}) %collective-permute-start.2) | collective-permute-done | bytes 131104 | tf_op jit(solution)/shard_map/ppermute | solution.py:430
  66.2 3.3 %shard_map.64 = bf16[8,2,4,128,128]{4,3,2,1,0:T(8,128)(2,1)} custom-call(s32[72]{0:T(128)} %concatenate.3.scal.refs_0_, bf16[4,128,128]{2,1,0:T(8,128)(2,1)} %copy-done.32, bf16[4,128,128]{2,1,0:T(8,128)(2,1)} %copy-done.31, bf16[4,128,128]{2,1,0:T(8,128)(2,1)} %copy-done.34, bf16[4,128,128]{2,1,0:T(8,128)(2,1)} %copy-done.33), custom_call_target="tpu_custom_call" | custom-call | bytes 1048576 | tf_op jit(solution)/shard_map/pallas_call | solution.py:140
  70.4 6.2 %all-to-all-start = ((bf16[8,2,4,128,128]{4,3,2,1,0:T(8,128)(2,1)}), bf16[8,2,4,128,128]{4,3,2,1,0:T(8,128)(2,1)S(1)}, u32[]{:S(2)}, u32[]{:S(2)}) async-start(bf16[8,2,4,128,128]{4,3,2,1,0:T(8,128)(2,1)} %shard_map.64), calls=%async_computation | async-start | bytes 4194304 | tf_op jit(solution)/shard_map/all_to_all | solution.py:440
  76.6 4.2 %shard_map.67 = (bf16[256,1024]{1,0:T(8,128)(2,1)}, bf16[256,1024]{1,0:T(8,128)(2,1)}, bf16[256,1024]{1,0:T(8,128)(2,1)}, bf16[256,1024]{1,0:T(8,128)(2,1)}) custom-call(s32[72]{0:T(128)} %concatenate.3.scal.refs_0_, f32[2048,1024]{1,0:T(8,128)} %bitcast.17), custom_call_target="tpu_custom_call" | custom-call | bytes 16777216 | tf_op jit(solution)/shard_map/pallas_call | solution.py:140
  80.8 3.9 %collective-permute-start.8 = (bf16[256,1024]{1,0:T(8,128)(2,1)}, bf16[256,1024]{1,0:T(8,128)(2,1)S(1)}, u32[]{:S(2)}, u32[]{:S(2)}) collective-permute-start(bf16[256,1024]{1,0:T(8,128)(2,1)} %get-tuple-element.32), channel_id=1, source_target_pairs={{0,2},{8,10},{16,18},{24,26},{32,34},{40,42},{48,50},{56,58},{64,6... | collective-permute-start | bytes 1572872 | tf_op jit(solution)/shard_map/ppermute | solution.py:398
  84.8 3.0 %collective-permute-start.9 = (bf16[256,1024]{1,0:T(8,128)(2,1)}, bf16[256,1024]{1,0:T(8,128)(2,1)}, u32[]{:S(2)}, u32[]{:S(2)}) collective-permute-start(bf16[256,1024]{1,0:T(8,128)(2,1)} %get-tuple-element.33), channel_id=1, source_target_pairs={{0,4},{8,12},{16,20},{24,28},{32,36},{40,44},{48,52},{56,60},{64,6... | collective-permute-start | bytes 1572872 | tf_op jit(solution)/shard_map/ppermute | solution.py:398
  96.2 15.5 %collective-permute-done.8 = bf16[256,1024]{1,0:T(8,128)(2,1)S(1)} collective-permute-done((bf16[256,1024]{1,0:T(8,128)(2,1)}, bf16[256,1024]{1,0:T(8,128)(2,1)S(1)}, u32[]{:S(2)}, u32[]{:S(2)}) %collective-permute-start.8) | collective-permute-done | bytes 524320 | tf_op jit(solution)/shard_map/ppermute | solution.py:398
  113.1 6.7 %collective-permute-done.9 = bf16[256,1024]{1,0:T(8,128)(2,1)} collective-permute-done((bf16[256,1024]{1,0:T(8,128)(2,1)}, bf16[256,1024]{1,0:T(8,128)(2,1)}, u32[]{:S(2)}, u32[]{:S(2)}) %collective-permute-start.9) | collective-permute-done | bytes 524320 | tf_op jit(solution)/shard_map/ppermute | solution.py:398
  130.8 4.9 %shard_map.70 = bf16[8,128,1024]{2,1,0:T(8,128)(2,1)} custom-call(s32[72]{0:T(128)} %concatenate.3.scal.refs_0_, bf16[256,1024]{1,0:T(8,128)(2,1)} %copy-done.7, bf16[128,1024]{1,0:T(8,128)(2,1)} %copy-done.23, bf16[8,2,4,128,128]{4,3,2,1,0:T(8,128)(2,1)} %copy-done.2, bf16[1024,128]{1,0:T(8,128)(2,1)} %get-tuple-element.35.refs_4_, ...), custom_call_target="tpu_custom_call" | custom-call | flops 134217728 | bytes 8126464 | tf_op jit(solution)/shard_map/pallas_call | solution.py:140
  135.7 12.9 %all-to-all-start.3 = ((bf16[8,128,1024]{2,1,0:T(8,128)(2,1)}), bf16[8,128,1024]{2,1,0:T(8,128)(2,1)S(1)}, u32[]{:S(2)}, u32[]{:S(2)}) async-start(bf16[8,128,1024]{2,1,0:T(8,128)(2,1)} %shard_map.70), calls=%async_computation.3 | async-start | bytes 4194304 | tf_op jit(solution)/shard_map/all_to_all | solution.py:453
  150.7 4.2 %shard_map.73 = (bf16[256,1024]{1,0:T(8,128)(2,1)}, bf16[256,1024]{1,0:T(8,128)(2,1)}, bf16[256,1024]{1,0:T(8,128)(2,1)}, bf16[256,1024]{1,0:T(8,128)(2,1)}) custom-call(s32[72]{0:T(128)} %concatenate.3.scal.refs_0_, f32[2048,1024]{1,0:T(8,128)} %bitcast.18), custom_call_target="tpu_custom_call" | custom-call | bytes 16777216 | tf_op jit(solution)/shard_map/pallas_call | solution.py:140
  154.9 3.9 %collective-permute-start.24 = (bf16[256,1024]{1,0:T(8,128)(2,1)}, bf16[256,1024]{1,0:T(8,128)(2,1)S(1)}, u32[]{:S(2)}, u32[]{:S(2)}) collective-permute-start(bf16[256,1024]{1,0:T(8,128)(2,1)} %get-tuple-element.39), channel_id=1, source_target_pairs={{0,2},{8,10},{16,18},{24,26},{32,34},{40,42},{48,50},{56,58},{64,6... | collective-permute-start | bytes 1572872 | tf_op jit(solution)/shard_map/ppermute | solution.py:398
  158.8 3.0 %collective-permute-start.25 = (bf16[256,1024]{1,0:T(8,128)(2,1)}, bf16[256,1024]{1,0:T(8,128)(2,1)}, u32[]{:S(2)}, u32[]{:S(2)}) collective-permute-start(bf16[256,1024]{1,0:T(8,128)(2,1)} %get-tuple-element.40), channel_id=1, source_target_pairs={{0,4},{8,12},{16,20},{24,28},{32,36},{40,44},{48,52},{56,60},{64,6... | collective-permute-start | bytes 1572872 | tf_op jit(solution)/shard_map/ppermute | solution.py:398
  165.3 12.4 %shard_map.71.tile = f32[2048,1024]{1,0:T(8,128)} custom-call(s32[72]{0:T(128)} %concatenate.3.scal.refs_0_, f32[2048,1024]{1,0:T(8,128)} %bitcast.19, bf16[8,2,4,128,128]{4,3,2,1,0:T(8,128)(2,1)} %copy-done.2, bf16[1024,128]{1,0:T(8,128)(2,1)} %get-tuple-element.36.v0, bf16[1024,128]{1,0:T(8,128)(2,1)} %copy-done.22, bf16[1024,128]{1,0:T(8,128)(2,1)} %copy-done.21, ...), custom_call_target="tpu_custom_call" | custom-call | flops 2147483648 | bytes 23068672 | tf_op jit(solution)/shard_map/pallas_call | solution.py:140
  179.1 16.5 %shard_map.72 = (f32[1024,1024]{1,0:T(8,128)}, bf16[1024,256]{1,0:T(8,128)(2,1)}, bf16[1024,256]{1,0:T(8,128)(2,1)}, bf16[1024,256]{1,0:T(8,128)(2,1)}, bf16[1024,256]{1,0:T(8,128)(2,1)}) custom-call(s32[72]{0:T(128)} %concatenate.3.scal.refs_0_, f32[2048,1024]{1,0:T(8,128)} %shard_map.71.tile, bf16[1024,1024]{1,0:T(8,128)(2,1)} %bitcast.20), custom_call_target="tpu_custom_call" | custom-call | flops 10737418240 | bytes 20971520 | tf_op jit(solution)/shard_map/pallas_call | solution.py:140
  200.3 5.6 %collective-permute-done.28 = bf16[1024,256]{1,0:T(8,128)(2,1)S(1)} collective-permute-done((bf16[1024,256]{1,0:T(8,128)(2,1)}, bf16[1024,256]{1,0:T(8,128)(2,1)S(1)}, u32[]{:S(2)}, u32[]{:S(2)}) %collective-permute-start.28) | collective-permute-done | bytes 524320 | tf_op jit(solution)/shard_map/ppermute | solution.py:468
  209.1 3.7 %collective-permute-start.30 = (bf16[1024,256]{1,0:T(8,128)(2,1)}, bf16[1024,256]{1,0:T(8,128)(2,1)}, u32[]{:S(2)}, u32[]{:S(2)}) collective-permute-start(bf16[1024,256]{1,0:T(8,128)(2,1)} %broadcast_select_fusion.3), channel_id=1, source_target_pairs={{0,8},{8,16},{1,9},{9,17},{2,10},{10,18},{3,11},{11,19},{4,12},{12... | collective-permute-start | bytes 1572872 | tf_op jit(solution)/shard_map/ppermute | solution.py:468
  212.8 4.0 %collective-permute-start.31 = (bf16[1024,256]{1,0:T(8,128)(2,1)}, bf16[1024,256]{1,0:T(8,128)(2,1)}, u32[]{:S(2)}, u32[]{:S(2)}) collective-permute-start(bf16[1024,256]{1,0:T(8,128)(2,1)} %broadcast_select_fusion.2), channel_id=1, source_target_pairs={{0,24},{24,16},{1,25},{25,17},{2,26},{26,18},{3,27},{27,19},{4,28}... | collective-permute-start | bytes 1572872 | tf_op jit(solution)/shard_map/ppermute | solution.py:471
  217.5 4.7 %shard_map.74 = bf16[8,128,1024]{2,1,0:T(8,128)(2,1)} custom-call(s32[72]{0:T(128)} %concatenate.3.scal.refs_0_, bf16[256,1024]{1,0:T(8,128)(2,1)} %copy-done.8, bf16[128,1024]{1,0:T(8,128)(2,1)} %copy-done.24, bf16[8,2,4,128,128]{4,3,2,1,0:T(8,128)(2,1)} %copy-done.2, bf16[1024,128]{1,0:T(8,128)(2,1)} %get-tuple-element.35.refs_4_, ...), custom_call_target="tpu_custom_call" | custom-call | flops 134217728 | bytes 7864320 | tf_op jit(solution)/shard_map/pallas_call | solution.py:140
  222.2 4.5 %all-to-all-start.4 = ((bf16[8,128,1024]{2,1,0:T(8,128)(2,1)}), bf16[8,128,1024]{2,1,0:T(8,128)(2,1)S(1)}, u32[]{:S(2)}, u32[]{:S(2)}) async-start(bf16[8,128,1024]{2,1,0:T(8,128)(2,1)} %shard_map.74), calls=%async_computation.4 | async-start | bytes 4194304 | tf_op jit(solution)/shard_map/all_to_all | solution.py:465
  230.1 4.1 %collective-permute-start.33 = (bf16[1024,256]{1,0:T(8,128)(2,1)}, bf16[1024,256]{1,0:T(8,128)(2,1)}, u32[]{:S(2)}, u32[]{:S(2)}) collective-permute-start(bf16[1024,256]{1,0:T(8,128)(2,1)} %get-tuple-element.53), channel_id=1, source_target_pairs={{0,24},{24,16},{16,8},{1,25},{25,17},{17,9},{2,26},{26,18},{18,10}... | collective-permute-start | bytes 1572872 | tf_op jit(solution)/shard_map/ppermute | solution.py:471
  240.7 3.6 %select_add_fusion = (bf16[1024,256]{1,0:T(8,128)(2,1)}, bf16[1024,256]{1,0:T(8,128)(2,1)}, bf16[1024,256]{1,0:T(8,128)(2,1)}, bf16[1024,256]{1,0:T(8,128)(2,1)}) fusion(bf16[1024,256]{1,0:T(8,128)(2,1)} %copy-done.12, bf16[1024,256]{1,0:T(8,128)(2,1)} %collective-permute-done.31, bf16[1024,256]{1,0:T(8,128)(2,1)} %collective-permute-done.33, ...), kind=kLoop, calls=%fused_computation | loop fusion | flops 7340032 | bytes 7340036 | tf_op jit(solution)/shard_map/add | solution.py:32
  245.5 7.3 %all-to-all-done.4 = bf16[8,128,1024]{2,1,0:T(8,128)(2,1)S(1)} async-done(((bf16[8,128,1024]{2,1,0:T(8,128)(2,1)}), bf16[8,128,1024]{2,1,0:T(8,128)(2,1)S(1)}, u32[]{:S(2)}, u32[]{:S(2)}) %all-to-all-start.4) | async-done | bytes 2097184 | tf_op jit(solution)/shard_map/all_to_all | solution.py:465
  254.1 12.3 %shard_map.75 = f32[2048,1024]{1,0:T(8,128)} custom-call(s32[72]{0:T(128)} %concatenate.3.scal.refs_0_, f32[2048,1024]{1,0:T(8,128)} %shard_map.71.tile, f32[1024,1024]{1,0:T(8,128)} %get-tuple-element.37.kc, bf16[1024,1024]{1,0:T(8,128)(2,1)} %bitcast.21, bf16[1024,1024]{1,0:T(8,128)(2,1)} %bitcast.22, bf16[1024,256]{1,0:T(8,128)(2,1)} %get-tuple-element.58.g0, ...), custom_call_target="tpu_custom_call" | custom-call | flops 4294967296 | bytes 38797312 | tf_op jit(solution)/shard_map/pallas_call | solution.py:140
  (164 shorter events, 71.4 us)
Async XLA Ops:
  13.9 32.0 %all-to-all-start.1 = ((bf16[8,128,256]{2,1,0:T(8,128)(2,1)}), bf16[8,128,256]{2,1,0:T(8,128)(2,1)S(1)}, u32[]{:S(2)}, u32[]{:S(2)}) async-start(bf16[8,128,256]{2,1,0:T(8,128)(2,1)} %shard_map.65), calls=%async_computation.1 | async-start | bytes 1048576 | tf_op jit(solution)/shard_map/all_to_all | solution.py:438
  20.2 14.6 %collective-permute-start.16 = (bf16[4,128,256]{2,1,0:T(8,128)(2,1)S(1)}, bf16[4,128,256]{2,1,0:T(8,128)(2,1)S(1)}, u32[]{:S(2)}, u32[]{:S(2)}) collective-permute-start(bf16[4,128,256]{2,1,0:T(8,128)(2,1)S(1)} %copy-done.41), channel_id=1, source_target_pairs={{0,40},{8,48},{16,56},{24,32},{32,72},{40,80},{48,88},{56,64},{64,... | collective-permute-start | bytes 786440 | tf_op jit(solution)/shard_map/ppermute | solution.py:430
  20.3 14.5 %collective-permute-start.15 = (bf16[4,128,256]{2,1,0:T(8,128)(2,1)S(1)}, bf16[4,128,256]{2,1,0:T(8,128)(2,1)S(1)}, u32[]{:S(2)}, u32[]{:S(2)}) collective-permute-start(bf16[4,128,256]{2,1,0:T(8,128)(2,1)S(1)} %copy-done.41), channel_id=1, source_target_pairs={{0,32},{8,40},{16,48},{24,56},{32,64},{40,72},{48,80},{56,88},{64,... | collective-permute-start | bytes 786440 | tf_op jit(solution)/shard_map/ppermute | solution.py:430
  22.7 14.0 %collective-permute-start.18 = (bf16[4,128,256]{2,1,0:T(8,128)(2,1)S(1)}, bf16[4,128,256]{2,1,0:T(8,128)(2,1)S(1)}, u32[]{:S(2)}, u32[]{:S(2)}) collective-permute-start(bf16[4,128,256]{2,1,0:T(8,128)(2,1)S(1)} %copy-done.41), channel_id=1, source_target_pairs={{0,56},{8,32},{16,40},{24,48},{32,88},{40,64},{48,72},{56,80},{64,... | collective-permute-start | bytes 786440 | tf_op jit(solution)/shard_map/ppermute | solution.py:430
  24.7 16.1 %collective-permute-start.17 = (bf16[4,128,256]{2,1,0:T(8,128)(2,1)S(1)}, bf16[4,128,256]{2,1,0:T(8,128)(2,1)S(1)}, u32[]{:S(2)}, u32[]{:S(2)}) collective-permute-start(bf16[4,128,256]{2,1,0:T(8,128)(2,1)S(1)} %copy-done.41), channel_id=1, source_target_pairs={{0,48},{8,56},{16,32},{24,40},{32,80},{40,88},{48,64},{56,72},{64,... | collective-permute-start | bytes 786440 | tf_op jit(solution)/shard_map/ppermute | solution.py:430
  45.9 23.7 %all-to-all-start.2 = ((bf16[8,128,256]{2,1,0:T(8,128)(2,1)}), bf16[8,128,256]{2,1,0:T(8,128)(2,1)S(1)}, u32[]{:S(2)}, u32[]{:S(2)}) async-start(bf16[8,128,256]{2,1,0:T(8,128)(2,1)} %shard_map.68), calls=%async_computation.2 | async-start | bytes 1048576 | tf_op jit(solution)/shard_map/all_to_all | solution.py:444
  52.2 9.0 %collective-permute-start.1 = (bf16[4,128,128]{2,1,0:T(8,128)(2,1)S(1)}, bf16[4,128,128]{2,1,0:T(8,128)(2,1)S(1)}, u32[]{:S(2)}, u32[]{:S(2)}) collective-permute-start(bf16[4,128,128]{2,1,0:T(8,128)(2,1)S(1)} %copy-done.42), channel_id=1, source_target_pairs={{0,40},{8,48},{16,56},{24,32},{32,72},{40,80},{48,88},{56,64},{64,... | collective-permute-start | bytes 393224 | tf_op jit(solution)/shard_map/ppermute | solution.py:430
  52.3 9.0 %collective-permute-start = (bf16[4,128,128]{2,1,0:T(8,128)(2,1)S(1)}, bf16[4,128,128]{2,1,0:T(8,128)(2,1)S(1)}, u32[]{:S(2)}, u32[]{:S(2)}) collective-permute-start(bf16[4,128,128]{2,1,0:T(8,128)(2,1)S(1)} %copy-done.42), channel_id=1, source_target_pairs={{0,32},{8,40},{16,48},{24,56},{32,64},{40,72},{48,80},{56,88},{64,... | collective-permute-start | bytes 393224 | tf_op jit(solution)/shard_map/ppermute | solution.py:430
  56.3 9.3 %collective-permute-start.2 = (bf16[4,128,128]{2,1,0:T(8,128)(2,1)S(1)}, bf16[4,128,128]{2,1,0:T(8,128)(2,1)S(1)}, u32[]{:S(2)}, u32[]{:S(2)}) collective-permute-start(bf16[4,128,128]{2,1,0:T(8,128)(2,1)S(1)} %copy-done.42), channel_id=1, source_target_pairs={{0,48},{8,56},{16,32},{24,40},{32,80},{40,88},{48,64},{56,72},{64,... | collective-permute-start | bytes 393224 | tf_op jit(solution)/shard_map/ppermute | solution.py:430
  70.4 58.5 %all-to-all-start = ((bf16[8,2,4,128,128]{4,3,2,1,0:T(8,128)(2,1)}), bf16[8,2,4,128,128]{4,3,2,1,0:T(8,128)(2,1)S(1)}, u32[]{:S(2)}, u32[]{:S(2)}) async-start(bf16[8,2,4,128,128]{4,3,2,1,0:T(8,128)(2,1)} %shard_map.64), calls=%async_computation | async-start | bytes 4194304 | tf_op jit(solution)/shard_map/all_to_all | solution.py:440
  80.8 30.9 %collective-permute-start.8 = (bf16[256,1024]{1,0:T(8,128)(2,1)}, bf16[256,1024]{1,0:T(8,128)(2,1)S(1)}, u32[]{:S(2)}, u32[]{:S(2)}) collective-permute-start(bf16[256,1024]{1,0:T(8,128)(2,1)} %get-tuple-element.32), channel_id=1, source_target_pairs={{0,2},{8,10},{16,18},{24,26},{32,34},{40,42},{48,50},{56,58},{64,6... | collective-permute-start | bytes 1572872 | tf_op jit(solution)/shard_map/ppermute | solution.py:398
  84.8 35.0 %collective-permute-start.9 = (bf16[256,1024]{1,0:T(8,128)(2,1)}, bf16[256,1024]{1,0:T(8,128)(2,1)}, u32[]{:S(2)}, u32[]{:S(2)}) collective-permute-start(bf16[256,1024]{1,0:T(8,128)(2,1)} %get-tuple-element.33), channel_id=1, source_target_pairs={{0,4},{8,12},{16,20},{24,28},{32,36},{40,44},{48,52},{56,60},{64,6... | collective-permute-start | bytes 1572872 | tf_op jit(solution)/shard_map/ppermute | solution.py:398
  87.7 32.1 %collective-permute-start.10 = (bf16[256,1024]{1,0:T(8,128)(2,1)}, bf16[256,1024]{1,0:T(8,128)(2,1)}, u32[]{:S(2)}, u32[]{:S(2)}) collective-permute-start(bf16[256,1024]{1,0:T(8,128)(2,1)} %get-tuple-element.34), channel_id=1, source_target_pairs={{0,6},{8,14},{16,22},{24,30},{32,38},{40,46},{48,54},{56,62},{64,7... | collective-permute-start | bytes 1572872 | tf_op jit(solution)/shard_map/ppermute | solution.py:398
  92.7 34.2 %collective-permute-start.14 = (bf16[1024,128]{1,0:T(8,128)(2,1)}, bf16[1024,128]{1,0:T(8,128)(2,1)S(1)}, u32[]{:S(2)}, u32[]{:S(2)}) collective-permute-start(bf16[1024,128]{1,0:T(8,128)(2,1)} %get-tuple-element.35.refs_4_), channel_id=1, source_target_pairs={{0,24},{8,0},{16,8},{24,16},{1,25},{9,1},{17,9},{25,17},{2,26},{10... | collective-permute-start | bytes 786440 | tf_op jit(solution)/shard_map/ppermute | solution.py:405
  95.1 32.5 %collective-permute-start.13 = (bf16[1024,128]{1,0:T(8,128)(2,1)}, bf16[1024,128]{1,0:T(8,128)(2,1)S(1)}, u32[]{:S(2)}, u32[]{:S(2)}) collective-permute-start(bf16[1024,128]{1,0:T(8,128)(2,1)} %get-tuple-element.35.refs_4_), channel_id=1, source_target_pairs={{0,16},{8,24},{16,0},{24,8},{1,17},{9,25},{17,1},{25,9},{2,18},{10... | collective-permute-start | bytes 786440 | tf_op jit(solution)/shard_map/ppermute | solution.py:405
  111.7 16.0 %collective-permute-start.12 = (bf16[1024,128]{1,0:T(8,128)(2,1)}, bf16[1024,128]{1,0:T(8,128)(2,1)S(1)}, u32[]{:S(2)}, u32[]{:S(2)}) collective-permute-start(bf16[1024,128]{1,0:T(8,128)(2,1)} %get-tuple-element.35.refs_4_), channel_id=1, source_target_pairs={{0,8},{8,16},{16,24},{24,0},{1,9},{9,17},{17,25},{25,1},{2,10},{10... | collective-permute-start | bytes 786440 | tf_op jit(solution)/shard_map/ppermute | solution.py:405
  135.7 42.1 %all-to-all-start.3 = ((bf16[8,128,1024]{2,1,0:T(8,128)(2,1)}), bf16[8,128,1024]{2,1,0:T(8,128)(2,1)S(1)}, u32[]{:S(2)}, u32[]{:S(2)}) async-start(bf16[8,128,1024]{2,1,0:T(8,128)(2,1)} %shard_map.70), calls=%async_computation.3 | async-start | bytes 4194304 | tf_op jit(solution)/shard_map/all_to_all | solution.py:453
  148.6 13.2 %collective-permute-start.23 = (bf16[1024,128]{1,0:T(8,128)(2,1)S(1)}, bf16[1024,128]{1,0:T(8,128)(2,1)S(1)}, u32[]{:S(2)}, u32[]{:S(2)}) collective-permute-start(bf16[1024,128]{1,0:T(8,128)(2,1)S(1)} %copy-done.19), channel_id=1, source_target_pairs={{0,24},{8,0},{16,8},{24,16},{1,25},{9,1},{17,9},{25,17},{2,26},{10... | collective-permute-start | bytes 786440 | tf_op jit(solution)/shard_map/ppermute | solution.py:405
  148.7 15.2 %collective-permute-start.22 = (bf16[1024,128]{1,0:T(8,128)(2,1)S(1)}, bf16[1024,128]{1,0:T(8,128)(2,1)S(1)}, u32[]{:S(2)}, u32[]{:S(2)}) collective-permute-start(bf16[1024,128]{1,0:T(8,128)(2,1)S(1)} %copy-done.19), channel_id=1, source_target_pairs={{0,16},{8,24},{16,0},{24,8},{1,17},{9,25},{17,1},{25,9},{2,18},{10... | collective-permute-start | bytes 786440 | tf_op jit(solution)/shard_map/ppermute | solution.py:405
  150.2 13.7 %collective-permute-start.21 = (bf16[1024,128]{1,0:T(8,128)(2,1)S(1)}, bf16[1024,128]{1,0:T(8,128)(2,1)S(1)}, u32[]{:S(2)}, u32[]{:S(2)}) collective-permute-start(bf16[1024,128]{1,0:T(8,128)(2,1)S(1)} %copy-done.19), channel_id=1, source_target_pairs={{0,8},{8,16},{16,24},{24,0},{1,9},{9,17},{17,25},{25,1},{2,10},{10... | collective-permute-start | bytes 786440 | tf_op jit(solution)/shard_map/ppermute | solution.py:405
  154.9 43.4 %collective-permute-start.24 = (bf16[256,1024]{1,0:T(8,128)(2,1)}, bf16[256,1024]{1,0:T(8,128)(2,1)S(1)}, u32[]{:S(2)}, u32[]{:S(2)}) collective-permute-start(bf16[256,1024]{1,0:T(8,128)(2,1)} %get-tuple-element.39), channel_id=1, source_target_pairs={{0,2},{8,10},{16,18},{24,26},{32,34},{40,42},{48,50},{56,58},{64,6... | collective-permute-start | bytes 1572872 | tf_op jit(solution)/shard_map/ppermute | solution.py:398
  158.8 39.5 %collective-permute-start.25 = (bf16[256,1024]{1,0:T(8,128)(2,1)}, bf16[256,1024]{1,0:T(8,128)(2,1)}, u32[]{:S(2)}, u32[]{:S(2)}) collective-permute-start(bf16[256,1024]{1,0:T(8,128)(2,1)} %get-tuple-element.40), channel_id=1, source_target_pairs={{0,4},{8,12},{16,20},{24,28},{32,36},{40,44},{48,52},{56,60},{64,6... | collective-permute-start | bytes 1572872 | tf_op jit(solution)/shard_map/ppermute | solution.py:398
  161.8 36.5 %collective-permute-start.26 = (bf16[256,1024]{1,0:T(8,128)(2,1)}, bf16[256,1024]{1,0:T(8,128)(2,1)}, u32[]{:S(2)}, u32[]{:S(2)}) collective-permute-start(bf16[256,1024]{1,0:T(8,128)(2,1)} %get-tuple-element.41), channel_id=1, source_target_pairs={{0,6},{8,14},{16,22},{24,30},{32,38},{40,46},{48,54},{56,62},{64,7... | collective-permute-start | bytes 1572872 | tf_op jit(solution)/shard_map/ppermute | solution.py:398
  195.5 10.4 %collective-permute-start.28 = (bf16[1024,256]{1,0:T(8,128)(2,1)}, bf16[1024,256]{1,0:T(8,128)(2,1)S(1)}, u32[]{:S(2)}, u32[]{:S(2)}) collective-permute-start(bf16[1024,256]{1,0:T(8,128)(2,1)} %get-tuple-element.42), channel_id=1, source_target_pairs={{0,8},{1,9},{2,10},{3,11},{4,12},{5,13},{6,14},{7,15},{32,40},{33,... | collective-permute-start | bytes 1572872 | tf_op jit(solution)/shard_map/ppermute | solution.py:468
  197.0 10.3 %collective-permute-start.29 = (bf16[1024,256]{1,0:T(8,128)(2,1)}, bf16[1024,256]{1,0:T(8,128)(2,1)S(1)}, u32[]{:S(2)}, u32[]{:S(2)}) collective-permute-start(bf16[1024,256]{1,0:T(8,128)(2,1)} %get-tuple-element.43), channel_id=1, source_target_pairs={{0,24},{1,25},{2,26},{3,27},{4,28},{5,29},{6,30},{7,31},{32,56},{3... | collective-permute-start | bytes 1572872 | tf_op jit(solution)/shard_map/ppermute | solution.py:471
  198.6 18.2 %collective-permute-start.27 = (bf16[128,1024]{1,0:T(8,128)(2,1)S(1)}, bf16[128,1024]{1,0:T(8,128)(2,1)S(1)}, u32[]{:S(2)}, u32[]{:S(2)}) collective-permute-start(bf16[128,1024]{1,0:T(8,128)(2,1)S(1)} %slice.27), channel_id=1, source_target_pairs={{0,1},{2,3},{4,5},{6,7},{8,9},{10,11},{12,13},{14,15},{16,17},{18,... | collective-permute-start | bytes 786440 | tf_op jit(solution)/shard_map/ppermute | solution.py:400
  209.1 17.7 %collective-permute-start.30 = (bf16[1024,256]{1,0:T(8,128)(2,1)}, bf16[1024,256]{1,0:T(8,128)(2,1)}, u32[]{:S(2)}, u32[]{:S(2)}) collective-permute-start(bf16[1024,256]{1,0:T(8,128)(2,1)} %broadcast_select_fusion.3), channel_id=1, source_target_pairs={{0,8},{8,16},{1,9},{9,17},{2,10},{10,18},{3,11},{11,19},{4,12},{12... | collective-permute-start | bytes 1572872 | tf_op jit(solution)/shard_map/ppermute | solution.py:468
  212.8 14.0 %collective-permute-start.31 = (bf16[1024,256]{1,0:T(8,128)(2,1)}, bf16[1024,256]{1,0:T(8,128)(2,1)}, u32[]{:S(2)}, u32[]{:S(2)}) collective-permute-start(bf16[1024,256]{1,0:T(8,128)(2,1)} %broadcast_select_fusion.2), channel_id=1, source_target_pairs={{0,24},{24,16},{1,25},{25,17},{2,26},{26,18},{3,27},{27,19},{4,28}... | collective-permute-start | bytes 1572872 | tf_op jit(solution)/shard_map/ppermute | solution.py:471
  222.2 30.6 %all-to-all-start.4 = ((bf16[8,128,1024]{2,1,0:T(8,128)(2,1)}), bf16[8,128,1024]{2,1,0:T(8,128)(2,1)S(1)}, u32[]{:S(2)}, u32[]{:S(2)}) async-start(bf16[8,128,1024]{2,1,0:T(8,128)(2,1)} %shard_map.74), calls=%async_computation.4 | async-start | bytes 4194304 | tf_op jit(solution)/shard_map/all_to_all | solution.py:465
  228.0 10.4 %collective-permute-start.32 = (bf16[1024,256]{1,0:T(8,128)(2,1)}, bf16[1024,256]{1,0:T(8,128)(2,1)}, u32[]{:S(2)}, u32[]{:S(2)}) collective-permute-start(bf16[1024,256]{1,0:T(8,128)(2,1)} %get-tuple-element.52), channel_id=1, source_target_pairs={{0,8},{8,16},{16,24},{1,9},{9,17},{17,25},{2,10},{10,18},{18,26},{... | collective-permute-start | bytes 1572872 | tf_op jit(solution)/shard_map/ppermute | solution.py:468
  230.1 10.7 %collective-permute-start.33 = (bf16[1024,256]{1,0:T(8,128)(2,1)}, bf16[1024,256]{1,0:T(8,128)(2,1)}, u32[]{:S(2)}, u32[]{:S(2)}) collective-permute-start(bf16[1024,256]{1,0:T(8,128)(2,1)} %get-tuple-element.53), channel_id=1, source_target_pairs={{0,24},{24,16},{16,8},{1,25},{25,17},{17,9},{2,26},{26,18},{18,10}... | collective-permute-start | bytes 1572872 | tf_op jit(solution)/shard_map/ppermute | solution.py:471
  234.2 10.1 %collective-permute-start.36 = (bf16[256,256]{1,0:T(8,128)(2,1)S(1)}, bf16[256,256]{1,0:T(8,128)(2,1)S(1)}, u32[]{:S(2)}, u32[]{:S(2)}) collective-permute-start(bf16[256,256]{1,0:T(8,128)(2,1)S(1)} %copy-done.13), channel_id=1, source_target_pairs={{8,0},{9,1},{18,10},{19,11},{28,20},{29,21},{6,30},{7,31},{40,32},... | collective-permute-start | bytes 393224 | tf_op jit(solution)/shard_map/ppermute | solution.py:462
  (53 other events, 360.8 us)
where the time goes:
time: 268 us; the launch traced here: 267 us
  starting transfers between devices  105 us (39%)
  Pallas kernels  74.6 us (28%)
  waiting for transfers between devices  66.2 us (25%)
  local copies, waits for them, and re-layouts  12.7 us (5%)
  other arithmetic  7.92 us (3%)
    pallas_call x12, Pallas kernels, call(): pl.pallas_call(kernel, out_shape=outs, grid_spec=pltpu.PrefetchScalarGrid...  74.6 us
    ppermute x12, waiting for transfers between devices, moved(): out.append(lax.ppermute(make(k), ('front', 'row'), pairs))  24.7 us
    ppermute x6, waiting for transfers between devices, spread(): lax.ppermute(pieces[i], COL, [(0, 2 * i)])  22.2 us
    ppermute x6, starting transfers between devices, spread(): lax.ppermute(pieces[i], COL, [(0, 2 * i)])  17.9 us
    ppermute x12, starting transfers between devices, moved(): out.append(lax.ppermute(make(k), ('front', 'row'), pairs))  17.8 us
    all_to_all x1, starting transfers between devices, local(): top = lax.all_to_all(slab_top, COL, 0, 0).reshape(K, K)  12.9 us
    unnamed x86, local copies, waits for them, and re-layouts  9.53 us
    ppermute x3, starting transfers between devices, down(): lax.ppermute(value, 'row', [(-i % 4, -(i + 1) % 4) for i in range(hops)])  9.45 us
  transfers between devices with their start and end apart: 42, of which 17 were waited for; matrix products, arithmetic and copies ran while one was open for 4% of the time, Pallas kernels for 21%

commit v1 on v0

--- a/solution.py
+++ b/solution.py
@@ -384,11 +384,13 @@
     rows, cols = tile.shape
     block = pl.BlockSpec((TALL, cols), lambda i, s: (i, 0))
     first = pl.BlockSpec((TALL, cols), lambda i, s: (jnp.minimum(i, 1), 0))
+    solved = pl.BlockSpec((TALL, cols), lambda i, s: (jnp.where(s[0] == 0, jnp.minimum(i, 1), 0), 0))
+    tiles = pl.BlockSpec((TALL, cols), lambda i, s: (jnp.where(s[0] == 0, jnp.maximum(i, 2), i), 0))
     second = pl.BlockSpec((TALL, cols), lambda i, s: (jnp.maximum(i, 2) - 2, 0))
     args = [tile, kc, top, low] + list(gs) + list(ds)
     return call(
         trail_kernel, scal, args,
-        [block, first, first, second] + [whole(x.shape) for x in args[4:]],
+        [tiles, solved, first, second] + [whole(x.shape) for x in args[4:]],
         shape(rows, cols, dtype=F32), block, grid=(rows // TALL,),
         flops=2 * rows * cols * K,
     )
@@ -439,7 +441,8 @@
     slots = simple(pick_left_kernel, scal, got_u, [shape(8, 2, 4, 128, rank)])[0]
     all_u = lax.all_to_all(after(slots, back_v[0, 0, 0]), COL, 0, 0)
     raw_top = spread(halve(scal, front, 0), y)
-    raw_low = spread(halve(scal, front, 1), y)
+    low_pieces = halve(scal, front, 1)
+    raw_low = spread(low_pieces, y)
     send = simple(pick_blocks_kernel, scal, got_d, [shape(8, 128, PANEL)])[0]
     back_d = lax.all_to_all(after(send, all_u[0, 0, 0, 0, 0]), COL, 0, 0)
     v_own, v_first = simple(place_right_kernel, scal, [back_v], [shape(K, rank), shape(K, rank)])
@@ -453,7 +456,7 @@
     top = lax.all_to_all(slab_top, COL, 0, 0).reshape(K, K)
     token = slab_top[0, 0, 0]
     slab_low = slab(scal, 1, raw_low, all_u, vs_first, ())
-    vs = over_rows(after(v_own, token))
+    vs = over_rows(v_own)
     ds = [d_mine]
     for s in range(1, 4):
         pairs = [

time: 268 us -> 267 us (level)
  no operation moved by 1% of the time
where the time goes in v1:
time: 267 us; the launch traced here: 265 us
  starting transfers between devices  105 us (39%)
  Pallas kernels  73.3 us (27%)
  waiting for transfers between devices  66.2 us (25%)
  local copies, waits for them, and re-layouts  12.7 us (5%)
  other arithmetic  7.92 us (3%)
    pallas_call x12, Pallas kernels, call(): pl.pallas_call(kernel, out_shape=outs, grid_spec=pltpu.PrefetchScalarGrid...  73.3 us
    ppermute x12, waiting for transfers between devices, moved(): out.append(lax.ppermute(make(k), ('front', 'row'), pairs))  24.7 us
    ppermute x6, waiting for transfers between devices, spread(): lax.ppermute(pieces[i], COL, [(0, 2 * i)])  22.2 us
    ppermute x6, starting transfers between devices, spread(): lax.ppermute(pieces[i], COL, [(0, 2 * i)])  17.9 us
    ppermute x12, starting transfers between devices, moved(): out.append(lax.ppermute(make(k), ('front', 'row'), pairs))  17.8 us
    all_to_all x1, starting transfers between devices, local(): top = lax.all_to_all(slab_top, COL, 0, 0).reshape(K, K)  12.9 us
    unnamed x86, local copies, waits for them, and re-layouts  9.53 us
    ppermute x3, starting transfers between devices, down(): lax.ppermute(value, 'row', [(-i % 4, -(i + 1) % 4) for i in range(hops)])  9.45 us
  transfers between devices with their start and end apart: 42, of which 17 were waited for; matrix products, arithmetic and copies ran while one was open for 4% of the time, Pallas kernels for 21%

profile of v1, /device:TPU:2, one launch (start us, length us, event | category | flops | bytes accessed | tf_op | source)
XLA Modules:
  0.0 265.3 jit_solution(17407312620309998808)
XLA Ops:
  0.9 3.5 %collective-permute-start.7 = (bf16[128,128]{1,0:T(8,128)(2,1)S(1)}, bf16[128,128]{1,0:T(8,128)(2,1)S(1)}, u32[]{:S(2)}, u32[]{:S(2)}) collective-permute-start(bf16[128,128]{1,0:T(8,128)(2,1)S(1)} %get-tuple-element.57), channel_id=1, source_target_pairs={{0,56},{8,32},{16,40},{24,48},{32,88},{40,64},{48,72},{56,80},{64,... | collective-permute-start | bytes 98312 | tf_op jit(solution)/shard_map/ppermute | solution.py:432
  13.9 6.3 %all-to-all-start.1 = ((bf16[8,128,256]{2,1,0:T(8,128)(2,1)}), bf16[8,128,256]{2,1,0:T(8,128)(2,1)S(1)}, u32[]{:S(2)}, u32[]{:S(2)}) async-start(bf16[8,128,256]{2,1,0:T(8,128)(2,1)} %shard_map.65), calls=%async_computation.1 | async-start | bytes 1048576 | tf_op jit(solution)/shard_map/all_to_all | solution.py:440
  25.6 9.2 %collective-permute-done.19.d1 = bf16[4,128,256]{2,1,0:T(8,128)(2,1)S(1)} collective-permute-done((bf16[4,128,256]{2,1,0:T(8,128)(2,1)S(1)}, bf16[4,128,256]{2,1,0:T(8,128)(2,1)S(1)}, u32[]{:S(2)}, u32[]{:S(2)}) %collective-permute-start.19) | collective-permute-done | bytes 262176 | tf_op jit(solution)/shard_map/ppermute | solution.py:432
  36.7 4.2 %collective-permute-done.20.d2 = bf16[4,128,256]{2,1,0:T(8,128)(2,1)S(1)} collective-permute-done((bf16[4,128,256]{2,1,0:T(8,128)(2,1)S(1)}, bf16[4,128,256]{2,1,0:T(8,128)(2,1)S(1)}, u32[]{:S(2)}, u32[]{:S(2)}) %collective-permute-start.20) | collective-permute-done | bytes 262176 | tf_op jit(solution)/shard_map/ppermute | solution.py:432
  41.5 4.3 %shard_map.69 = bf16[8,128,256]{2,1,0:T(8,128)(2,1)} custom-call(s32[72]{0:T(128)} %concatenate.3.scal.refs_0_, bf16[4,128,256]{2,1,0:T(8,128)(2,1)} %copy-done.26, bf16[4,128,256]{2,1,0:T(8,128)(2,1)} %copy-done.25, bf16[4,128,256]{2,1,0:T(8,128)(2,1)} %copy-done.28, bf16[4,128,256]{2,1,0:T(8,128)(2,1)} %copy-done.27), custom_call_target="tpu_custom_call" | custom-call | bytes 2097152 | tf_op jit(solution)/shard_map/pallas_call | solution.py:140
  45.9 6.3 %all-to-all-start.2 = ((bf16[8,128,256]{2,1,0:T(8,128)(2,1)}), bf16[8,128,256]{2,1,0:T(8,128)(2,1)S(1)}, u32[]{:S(2)}, u32[]{:S(2)}) async-start(bf16[8,128,256]{2,1,0:T(8,128)(2,1)} %shard_map.69), calls=%async_computation.2 | async-start | bytes 1048576 | tf_op jit(solution)/shard_map/all_to_all | solution.py:447
  52.3 3.6 %collective-permute-start = (bf16[4,128,128]{2,1,0:T(8,128)(2,1)S(1)}, bf16[4,128,128]{2,1,0:T(8,128)(2,1)S(1)}, u32[]{:S(2)}, u32[]{:S(2)}) collective-permute-start(bf16[4,128,128]{2,1,0:T(8,128)(2,1)S(1)} %copy-done.42), channel_id=1, source_target_pairs={{0,32},{8,40},{16,48},{24,56},{32,64},{40,72},{48,80},{56,88},{64,... | collective-permute-start | bytes 393224 | tf_op jit(solution)/shard_map/ppermute | solution.py:432
  57.7 3.5 %collective-permute-done.1.u1 = bf16[4,128,128]{2,1,0:T(8,128)(2,1)S(1)} collective-permute-done((bf16[4,128,128]{2,1,0:T(8,128)(2,1)S(1)}, bf16[4,128,128]{2,1,0:T(8,128)(2,1)S(1)}, u32[]{:S(2)}, u32[]{:S(2)}) %collective-permute-start.1) | collective-permute-done | bytes 131104 | tf_op jit(solution)/shard_map/ppermute | solution.py:432
  62.5 3.0 %collective-permute-done.2.u2 = bf16[4,128,128]{2,1,0:T(8,128)(2,1)S(1)} collective-permute-done((bf16[4,128,128]{2,1,0:T(8,128)(2,1)S(1)}, bf16[4,128,128]{2,1,0:T(8,128)(2,1)S(1)}, u32[]{:S(2)}, u32[]{:S(2)}) %collective-permute-start.2) | collective-permute-done | bytes 131104 | tf_op jit(solution)/shard_map/ppermute | solution.py:432
  66.2 3.3 %shard_map.64 = bf16[8,2,4,128,128]{4,3,2,1,0:T(8,128)(2,1)} custom-call(s32[72]{0:T(128)} %concatenate.3.scal.refs_0_, bf16[4,128,128]{2,1,0:T(8,128)(2,1)} %copy-done.32, bf16[4,128,128]{2,1,0:T(8,128)(2,1)} %copy-done.31, bf16[4,128,128]{2,1,0:T(8,128)(2,1)} %copy-done.34, bf16[4,128,128]{2,1,0:T(8,128)(2,1)} %copy-done.33), custom_call_target="tpu_custom_call" | custom-call | bytes 1048576 | tf_op jit(solution)/shard_map/pallas_call | solution.py:140
  70.4 6.2 %all-to-all-start = ((bf16[8,2,4,128,128]{4,3,2,1,0:T(8,128)(2,1)}), bf16[8,2,4,128,128]{4,3,2,1,0:T(8,128)(2,1)S(1)}, u32[]{:S(2)}, u32[]{:S(2)}) async-start(bf16[8,2,4,128,128]{4,3,2,1,0:T(8,128)(2,1)} %shard_map.64), calls=%async_computation | async-start | bytes 4194304 | tf_op jit(solution)/shard_map/all_to_all | solution.py:442
  76.6 4.2 %shard_map.68 = (bf16[256,1024]{1,0:T(8,128)(2,1)}, bf16[256,1024]{1,0:T(8,128)(2,1)}, bf16[256,1024]{1,0:T(8,128)(2,1)}, bf16[256,1024]{1,0:T(8,128)(2,1)}) custom-call(s32[72]{0:T(128)} %concatenate.3.scal.refs_0_, f32[2048,1024]{1,0:T(8,128)} %bitcast.16), custom_call_target="tpu_custom_call" | custom-call | bytes 16777216 | tf_op jit(solution)/shard_map/pallas_call | solution.py:140
  80.8 3.9 %collective-permute-start.11 = (bf16[256,1024]{1,0:T(8,128)(2,1)}, bf16[256,1024]{1,0:T(8,128)(2,1)S(1)}, u32[]{:S(2)}, u32[]{:S(2)}) collective-permute-start(bf16[256,1024]{1,0:T(8,128)(2,1)} %get-tuple-element.30), channel_id=1, source_target_pairs={{0,2},{8,10},{16,18},{24,26},{32,34},{40,42},{48,50},{56,58},{64,6... | collective-permute-start | bytes 1572872 | tf_op jit(solution)/shard_map/ppermute | solution.py:400
  84.8 3.0 %collective-permute-start.12 = (bf16[256,1024]{1,0:T(8,128)(2,1)}, bf16[256,1024]{1,0:T(8,128)(2,1)}, u32[]{:S(2)}, u32[]{:S(2)}) collective-permute-start(bf16[256,1024]{1,0:T(8,128)(2,1)} %get-tuple-element.31), channel_id=1, source_target_pairs={{0,4},{8,12},{16,20},{24,28},{32,36},{40,44},{48,52},{56,60},{64,6... | collective-permute-start | bytes 1572872 | tf_op jit(solution)/shard_map/ppermute | solution.py:400
  96.2 15.5 %collective-permute-done.11 = bf16[256,1024]{1,0:T(8,128)(2,1)S(1)} collective-permute-done((bf16[256,1024]{1,0:T(8,128)(2,1)}, bf16[256,1024]{1,0:T(8,128)(2,1)S(1)}, u32[]{:S(2)}, u32[]{:S(2)}) %collective-permute-start.11) | collective-permute-done | bytes 524320 | tf_op jit(solution)/shard_map/ppermute | solution.py:400
  113.1 6.7 %collective-permute-done.12 = bf16[256,1024]{1,0:T(8,128)(2,1)} collective-permute-done((bf16[256,1024]{1,0:T(8,128)(2,1)}, bf16[256,1024]{1,0:T(8,128)(2,1)}, u32[]{:S(2)}, u32[]{:S(2)}) %collective-permute-start.12) | collective-permute-done | bytes 524320 | tf_op jit(solution)/shard_map/ppermute | solution.py:400
  130.8 4.9 %shard_map.71 = bf16[8,128,1024]{2,1,0:T(8,128)(2,1)} custom-call(s32[72]{0:T(128)} %concatenate.3.scal.refs_0_, bf16[256,1024]{1,0:T(8,128)(2,1)} %copy-done.7, bf16[128,1024]{1,0:T(8,128)(2,1)} %copy-done.23, bf16[8,2,4,128,128]{4,3,2,1,0:T(8,128)(2,1)} %copy-done.2, bf16[1024,128]{1,0:T(8,128)(2,1)} %get-tuple-element.33.refs_4_, ...), custom_call_target="tpu_custom_call" | custom-call | flops 134217728 | bytes 8126464 | tf_op jit(solution)/shard_map/pallas_call | solution.py:140
  135.7 12.9 %all-to-all-start.3 = ((bf16[8,128,1024]{2,1,0:T(8,128)(2,1)}), bf16[8,128,1024]{2,1,0:T(8,128)(2,1)S(1)}, u32[]{:S(2)}, u32[]{:S(2)}) async-start(bf16[8,128,1024]{2,1,0:T(8,128)(2,1)} %shard_map.71), calls=%async_computation.3 | async-start | bytes 4194304 | tf_op jit(solution)/shard_map/all_to_all | solution.py:456
  150.7 4.2 %shard_map.73 = (bf16[256,1024]{1,0:T(8,128)(2,1)}, bf16[256,1024]{1,0:T(8,128)(2,1)}, bf16[256,1024]{1,0:T(8,128)(2,1)}, bf16[256,1024]{1,0:T(8,128)(2,1)}) custom-call(s32[72]{0:T(128)} %concatenate.3.scal.refs_0_, f32[2048,1024]{1,0:T(8,128)} %bitcast.17), custom_call_target="tpu_custom_call" | custom-call | bytes 16777216 | tf_op jit(solution)/shard_map/pallas_call | solution.py:140
  154.9 3.9 %collective-permute-start.24 = (bf16[256,1024]{1,0:T(8,128)(2,1)}, bf16[256,1024]{1,0:T(8,128)(2,1)S(1)}, u32[]{:S(2)}, u32[]{:S(2)}) collective-permute-start(bf16[256,1024]{1,0:T(8,128)(2,1)} %get-tuple-element.36), channel_id=1, source_target_pairs={{0,2},{8,10},{16,18},{24,26},{32,34},{40,42},{48,50},{56,58},{64,6... | collective-permute-start | bytes 1572872 | tf_op jit(solution)/shard_map/ppermute | solution.py:400
  158.8 3.0 %collective-permute-start.25 = (bf16[256,1024]{1,0:T(8,128)(2,1)}, bf16[256,1024]{1,0:T(8,128)(2,1)}, u32[]{:S(2)}, u32[]{:S(2)}) collective-permute-start(bf16[256,1024]{1,0:T(8,128)(2,1)} %get-tuple-element.37), channel_id=1, source_target_pairs={{0,4},{8,12},{16,20},{24,28},{32,36},{40,44},{48,52},{56,60},{64,6... | collective-permute-start | bytes 1572872 | tf_op jit(solution)/shard_map/ppermute | solution.py:400
  165.3 12.4 %shard_map.67.tile = f32[2048,1024]{1,0:T(8,128)} custom-call(s32[72]{0:T(128)} %concatenate.3.scal.refs_0_, f32[2048,1024]{1,0:T(8,128)} %bitcast.18, bf16[8,2,4,128,128]{4,3,2,1,0:T(8,128)(2,1)} %copy-done.2, bf16[1024,128]{1,0:T(8,128)(2,1)} %get-tuple-element.28.v0, bf16[1024,128]{1,0:T(8,128)(2,1)} %copy-done.22, bf16[1024,128]{1,0:T(8,128)(2,1)} %copy-done.21, ...), custom_call_target="tpu_custom_call" | custom-call | flops 2147483648 | bytes 23068672 | tf_op jit(solution)/shard_map/pallas_call | solution.py:140
  179.1 16.5 %shard_map.72 = (f32[1024,1024]{1,0:T(8,128)}, bf16[1024,256]{1,0:T(8,128)(2,1)}, bf16[1024,256]{1,0:T(8,128)(2,1)}, bf16[1024,256]{1,0:T(8,128)(2,1)}, bf16[1024,256]{1,0:T(8,128)(2,1)}) custom-call(s32[72]{0:T(128)} %concatenate.3.scal.refs_0_, f32[2048,1024]{1,0:T(8,128)} %shard_map.67.tile, bf16[1024,1024]{1,0:T(8,128)(2,1)} %bitcast.19), custom_call_target="tpu_custom_call" | custom-call | flops 10737418240 | bytes 20971520 | tf_op jit(solution)/shard_map/pallas_call | solution.py:140
  200.3 5.6 %collective-permute-done.28 = bf16[1024,256]{1,0:T(8,128)(2,1)S(1)} collective-permute-done((bf16[1024,256]{1,0:T(8,128)(2,1)}, bf16[1024,256]{1,0:T(8,128)(2,1)S(1)}, u32[]{:S(2)}, u32[]{:S(2)}) %collective-permute-start.28) | collective-permute-done | bytes 524320 | tf_op jit(solution)/shard_map/ppermute | solution.py:471
  209.1 3.7 %collective-permute-start.30 = (bf16[1024,256]{1,0:T(8,128)(2,1)}, bf16[1024,256]{1,0:T(8,128)(2,1)}, u32[]{:S(2)}, u32[]{:S(2)}) collective-permute-start(bf16[1024,256]{1,0:T(8,128)(2,1)} %broadcast_select_fusion.3), channel_id=1, source_target_pairs={{0,8},{8,16},{1,9},{9,17},{2,10},{10,18},{3,11},{11,19},{4,12},{12... | collective-permute-start | bytes 1572872 | tf_op jit(solution)/shard_map/ppermute | solution.py:471
  212.8 4.0 %collective-permute-start.31 = (bf16[1024,256]{1,0:T(8,128)(2,1)}, bf16[1024,256]{1,0:T(8,128)(2,1)}, u32[]{:S(2)}, u32[]{:S(2)}) collective-permute-start(bf16[1024,256]{1,0:T(8,128)(2,1)} %broadcast_select_fusion.2), channel_id=1, source_target_pairs={{0,24},{24,16},{1,25},{25,17},{2,26},{26,18},{3,27},{27,19},{4,28}... | collective-permute-start | bytes 1572872 | tf_op jit(solution)/shard_map/ppermute | solution.py:474
  217.5 4.7 %shard_map.74 = bf16[8,128,1024]{2,1,0:T(8,128)(2,1)} custom-call(s32[72]{0:T(128)} %concatenate.3.scal.refs_0_, bf16[256,1024]{1,0:T(8,128)(2,1)} %copy-done.8, bf16[128,1024]{1,0:T(8,128)(2,1)} %copy-done.24, bf16[8,2,4,128,128]{4,3,2,1,0:T(8,128)(2,1)} %copy-done.2, bf16[1024,128]{1,0:T(8,128)(2,1)} %get-tuple-element.33.refs_4_, ...), custom_call_target="tpu_custom_call" | custom-call | flops 134217728 | bytes 7864320 | tf_op jit(solution)/shard_map/pallas_call | solution.py:140
  222.2 4.5 %all-to-all-start.4 = ((bf16[8,128,1024]{2,1,0:T(8,128)(2,1)}), bf16[8,128,1024]{2,1,0:T(8,128)(2,1)S(1)}, u32[]{:S(2)}, u32[]{:S(2)}) async-start(bf16[8,128,1024]{2,1,0:T(8,128)(2,1)} %shard_map.74), calls=%async_computation.4 | async-start | bytes 4194304 | tf_op jit(solution)/shard_map/all_to_all | solution.py:468
  230.1 4.1 %collective-permute-start.33 = (bf16[1024,256]{1,0:T(8,128)(2,1)}, bf16[1024,256]{1,0:T(8,128)(2,1)}, u32[]{:S(2)}, u32[]{:S(2)}) collective-permute-start(bf16[1024,256]{1,0:T(8,128)(2,1)} %get-tuple-element.50), channel_id=1, source_target_pairs={{0,24},{24,16},{16,8},{1,25},{25,17},{17,9},{2,26},{26,18},{18,10}... | collective-permute-start | bytes 1572872 | tf_op jit(solution)/shard_map/ppermute | solution.py:474
  240.7 3.6 %select_add_fusion = (bf16[1024,256]{1,0:T(8,128)(2,1)}, bf16[1024,256]{1,0:T(8,128)(2,1)}, bf16[1024,256]{1,0:T(8,128)(2,1)}, bf16[1024,256]{1,0:T(8,128)(2,1)}) fusion(bf16[1024,256]{1,0:T(8,128)(2,1)} %copy-done.12, bf16[1024,256]{1,0:T(8,128)(2,1)} %collective-permute-done.31, bf16[1024,256]{1,0:T(8,128)(2,1)} %collective-permute-done.33, ...), kind=kLoop, calls=%fused_computation | loop fusion | flops 7340032 | bytes 7340036 | tf_op jit(solution)/shard_map/add | solution.py:32
  245.5 7.3 %all-to-all-done.4 = bf16[8,128,1024]{2,1,0:T(8,128)(2,1)S(1)} async-done(((bf16[8,128,1024]{2,1,0:T(8,128)(2,1)}), bf16[8,128,1024]{2,1,0:T(8,128)(2,1)S(1)}, u32[]{:S(2)}, u32[]{:S(2)}) %all-to-all-start.4) | async-done | bytes 2097184 | tf_op jit(solution)/shard_map/all_to_all | solution.py:468
  254.1 11.0 %shard_map.75 = f32[2048,1024]{1,0:T(8,128)} custom-call(s32[72]{0:T(128)} %concatenate.3.scal.refs_0_, f32[2048,1024]{1,0:T(8,128)} %shard_map.67.tile, f32[1024,1024]{1,0:T(8,128)} %get-tuple-element.34.kc, bf16[1024,1024]{1,0:T(8,128)(2,1)} %bitcast.20, bf16[1024,1024]{1,0:T(8,128)(2,1)} %bitcast.21, bf16[1024,256]{1,0:T(8,128)(2,1)} %get-tuple-element.54.g0, ...), custom_call_target="tpu_custom_call" | custom-call | flops 4294967296 | bytes 38797312 | tf_op jit(solution)/shard_map/pallas_call | solution.py:140
  (164 shorter events, 71.4 us)
Async XLA Ops:
  13.9 32.0 %all-to-all-start.1 = ((bf16[8,128,256]{2,1,0:T(8,128)(2,1)}), bf16[8,128,256]{2,1,0:T(8,128)(2,1)S(1)}, u32[]{:S(2)}, u32[]{:S(2)}) async-start(bf16[8,128,256]{2,1,0:T(8,128)(2,1)} %shard_map.65), calls=%async_computation.1 | async-start | bytes 1048576 | tf_op jit(solution)/shard_map/all_to_all | solution.py:440
  20.2 14.6 %collective-permute-start.19 = (bf16[4,128,256]{2,1,0:T(8,128)(2,1)S(1)}, bf16[4,128,256]{2,1,0:T(8,128)(2,1)S(1)}, u32[]{:S(2)}, u32[]{:S(2)}) collective-permute-start(bf16[4,128,256]{2,1,0:T(8,128)(2,1)S(1)} %copy-done.41), channel_id=1, source_target_pairs={{0,40},{8,48},{16,56},{24,32},{32,72},{40,80},{48,88},{56,64},{64,... | collective-permute-start | bytes 786440 | tf_op jit(solution)/shard_map/ppermute | solution.py:432
  20.3 14.5 %collective-permute-start.18 = (bf16[4,128,256]{2,1,0:T(8,128)(2,1)S(1)}, bf16[4,128,256]{2,1,0:T(8,128)(2,1)S(1)}, u32[]{:S(2)}, u32[]{:S(2)}) collective-permute-start(bf16[4,128,256]{2,1,0:T(8,128)(2,1)S(1)} %copy-done.41), channel_id=1, source_target_pairs={{0,32},{8,40},{16,48},{24,56},{32,64},{40,72},{48,80},{56,88},{64,... | collective-permute-start | bytes 786440 | tf_op jit(solution)/shard_map/ppermute | solution.py:432
  22.7 14.0 %collective-permute-start.21 = (bf16[4,128,256]{2,1,0:T(8,128)(2,1)S(1)}, bf16[4,128,256]{2,1,0:T(8,128)(2,1)S(1)}, u32[]{:S(2)}, u32[]{:S(2)}) collective-permute-start(bf16[4,128,256]{2,1,0:T(8,128)(2,1)S(1)} %copy-done.41), channel_id=1, source_target_pairs={{0,56},{8,32},{16,40},{24,48},{32,88},{40,64},{48,72},{56,80},{64,... | collective-permute-start | bytes 786440 | tf_op jit(solution)/shard_map/ppermute | solution.py:432
  24.7 16.1 %collective-permute-start.20 = (bf16[4,128,256]{2,1,0:T(8,128)(2,1)S(1)}, bf16[4,128,256]{2,1,0:T(8,128)(2,1)S(1)}, u32[]{:S(2)}, u32[]{:S(2)}) collective-permute-start(bf16[4,128,256]{2,1,0:T(8,128)(2,1)S(1)} %copy-done.41), channel_id=1, source_target_pairs={{0,48},{8,56},{16,32},{24,40},{32,80},{40,88},{48,64},{56,72},{64,... | collective-permute-start | bytes 786440 | tf_op jit(solution)/shard_map/ppermute | solution.py:432
  45.9 23.7 %all-to-all-start.2 = ((bf16[8,128,256]{2,1,0:T(8,128)(2,1)}), bf16[8,128,256]{2,1,0:T(8,128)(2,1)S(1)}, u32[]{:S(2)}, u32[]{:S(2)}) async-start(bf16[8,128,256]{2,1,0:T(8,128)(2,1)} %shard_map.69), calls=%async_computation.2 | async-start | bytes 1048576 | tf_op jit(solution)/shard_map/all_to_all | solution.py:447
  52.2 9.0 %collective-permute-start.1 = (bf16[4,128,128]{2,1,0:T(8,128)(2,1)S(1)}, bf16[4,128,128]{2,1,0:T(8,128)(2,1)S(1)}, u32[]{:S(2)}, u32[]{:S(2)}) collective-permute-start(bf16[4,128,128]{2,1,0:T(8,128)(2,1)S(1)} %copy-done.42), channel_id=1, source_target_pairs={{0,40},{8,48},{16,56},{24,32},{32,72},{40,80},{48,88},{56,64},{64,... | collective-permute-start | bytes 393224 | tf_op jit(solution)/shard_map/ppermute | solution.py:432
  52.3 9.0 %collective-permute-start = (bf16[4,128,128]{2,1,0:T(8,128)(2,1)S(1)}, bf16[4,128,128]{2,1,0:T(8,128)(2,1)S(1)}, u32[]{:S(2)}, u32[]{:S(2)}) collective-permute-start(bf16[4,128,128]{2,1,0:T(8,128)(2,1)S(1)} %copy-done.42), channel_id=1, source_target_pairs={{0,32},{8,40},{16,48},{24,56},{32,64},{40,72},{48,80},{56,88},{64,... | collective-permute-start | bytes 393224 | tf_op jit(solution)/shard_map/ppermute | solution.py:432
  56.3 9.3 %collective-permute-start.2 = (bf16[4,128,128]{2,1,0:T(8,128)(2,1)S(1)}, bf16[4,128,128]{2,1,0:T(8,128)(2,1)S(1)}, u32[]{:S(2)}, u32[]{:S(2)}) collective-permute-start(bf16[4,128,128]{2,1,0:T(8,128)(2,1)S(1)} %copy-done.42), channel_id=1, source_target_pairs={{0,48},{8,56},{16,32},{24,40},{32,80},{40,88},{48,64},{56,72},{64,... | collective-permute-start | bytes 393224 | tf_op jit(solution)/shard_map/ppermute | solution.py:432
  70.4 58.5 %all-to-all-start = ((bf16[8,2,4,128,128]{4,3,2,1,0:T(8,128)(2,1)}), bf16[8,2,4,128,128]{4,3,2,1,0:T(8,128)(2,1)S(1)}, u32[]{:S(2)}, u32[]{:S(2)}) async-start(bf16[8,2,4,128,128]{4,3,2,1,0:T(8,128)(2,1)} %shard_map.64), calls=%async_computation | async-start | bytes 4194304 | tf_op jit(solution)/shard_map/all_to_all | solution.py:442
  80.8 30.9 %collective-permute-start.11 = (bf16[256,1024]{1,0:T(8,128)(2,1)}, bf16[256,1024]{1,0:T(8,128)(2,1)S(1)}, u32[]{:S(2)}, u32[]{:S(2)}) collective-permute-start(bf16[256,1024]{1,0:T(8,128)(2,1)} %get-tuple-element.30), channel_id=1, source_target_pairs={{0,2},{8,10},{16,18},{24,26},{32,34},{40,42},{48,50},{56,58},{64,6... | collective-permute-start | bytes 1572872 | tf_op jit(solution)/shard_map/ppermute | solution.py:400
  84.8 35.0 %collective-permute-start.12 = (bf16[256,1024]{1,0:T(8,128)(2,1)}, bf16[256,1024]{1,0:T(8,128)(2,1)}, u32[]{:S(2)}, u32[]{:S(2)}) collective-permute-start(bf16[256,1024]{1,0:T(8,128)(2,1)} %get-tuple-element.31), channel_id=1, source_target_pairs={{0,4},{8,12},{16,20},{24,28},{32,36},{40,44},{48,52},{56,60},{64,6... | collective-permute-start | bytes 1572872 | tf_op jit(solution)/shard_map/ppermute | solution.py:400
  87.7 32.1 %collective-permute-start.13 = (bf16[256,1024]{1,0:T(8,128)(2,1)}, bf16[256,1024]{1,0:T(8,128)(2,1)}, u32[]{:S(2)}, u32[]{:S(2)}) collective-permute-start(bf16[256,1024]{1,0:T(8,128)(2,1)} %get-tuple-element.32), channel_id=1, source_target_pairs={{0,6},{8,14},{16,22},{24,30},{32,38},{40,46},{48,54},{56,62},{64,7... | collective-permute-start | bytes 1572872 | tf_op jit(solution)/shard_map/ppermute | solution.py:400
  92.7 34.2 %collective-permute-start.17 = (bf16[1024,128]{1,0:T(8,128)(2,1)}, bf16[1024,128]{1,0:T(8,128)(2,1)S(1)}, u32[]{:S(2)}, u32[]{:S(2)}) collective-permute-start(bf16[1024,128]{1,0:T(8,128)(2,1)} %get-tuple-element.33.refs_4_), channel_id=1, source_target_pairs={{0,24},{8,0},{16,8},{24,16},{1,25},{9,1},{17,9},{25,17},{2,26},{10... | collective-permute-start | bytes 786440 | tf_op jit(solution)/shard_map/ppermute | solution.py:407
  95.1 32.5 %collective-permute-start.16 = (bf16[1024,128]{1,0:T(8,128)(2,1)}, bf16[1024,128]{1,0:T(8,128)(2,1)S(1)}, u32[]{:S(2)}, u32[]{:S(2)}) collective-permute-start(bf16[1024,128]{1,0:T(8,128)(2,1)} %get-tuple-element.33.refs_4_), channel_id=1, source_target_pairs={{0,16},{8,24},{16,0},{24,8},{1,17},{9,25},{17,1},{25,9},{2,18},{10... | collective-permute-start | bytes 786440 | tf_op jit(solution)/shard_map/ppermute | solution.py:407
  111.7 16.0 %collective-permute-start.15 = (bf16[1024,128]{1,0:T(8,128)(2,1)}, bf16[1024,128]{1,0:T(8,128)(2,1)S(1)}, u32[]{:S(2)}, u32[]{:S(2)}) collective-permute-start(bf16[1024,128]{1,0:T(8,128)(2,1)} %get-tuple-element.33.refs_4_), channel_id=1, source_target_pairs={{0,8},{8,16},{16,24},{24,0},{1,9},{9,17},{17,25},{25,1},{2,10},{10... | collective-permute-start | bytes 786440 | tf_op jit(solution)/shard_map/ppermute | solution.py:407
  135.7 42.1 %all-to-all-start.3 = ((bf16[8,128,1024]{2,1,0:T(8,128)(2,1)}), bf16[8,128,1024]{2,1,0:T(8,128)(2,1)S(1)}, u32[]{:S(2)}, u32[]{:S(2)}) async-start(bf16[8,128,1024]{2,1,0:T(8,128)(2,1)} %shard_map.71), calls=%async_computation.3 | async-start | bytes 4194304 | tf_op jit(solution)/shard_map/all_to_all | solution.py:456
  148.6 13.2 %collective-permute-start.10 = (bf16[1024,128]{1,0:T(8,128)(2,1)S(1)}, bf16[1024,128]{1,0:T(8,128)(2,1)S(1)}, u32[]{:S(2)}, u32[]{:S(2)}) collective-permute-start(bf16[1024,128]{1,0:T(8,128)(2,1)S(1)} %copy-done.19), channel_id=1, source_target_pairs={{0,24},{8,0},{16,8},{24,16},{1,25},{9,1},{17,9},{25,17},{2,26},{10... | collective-permute-start | bytes 786440 | tf_op jit(solution)/shard_map/ppermute | solution.py:407
  148.7 15.2 %collective-permute-start.9 = (bf16[1024,128]{1,0:T(8,128)(2,1)S(1)}, bf16[1024,128]{1,0:T(8,128)(2,1)S(1)}, u32[]{:S(2)}, u32[]{:S(2)}) collective-permute-start(bf16[1024,128]{1,0:T(8,128)(2,1)S(1)} %copy-done.19), channel_id=1, source_target_pairs={{0,16},{8,24},{16,0},{24,8},{1,17},{9,25},{17,1},{25,9},{2,18},{10... | collective-permute-start | bytes 786440 | tf_op jit(solution)/shard_map/ppermute | solution.py:407
  150.2 13.7 %collective-permute-start.8 = (bf16[1024,128]{1,0:T(8,128)(2,1)S(1)}, bf16[1024,128]{1,0:T(8,128)(2,1)S(1)}, u32[]{:S(2)}, u32[]{:S(2)}) collective-permute-start(bf16[1024,128]{1,0:T(8,128)(2,1)S(1)} %copy-done.19), channel_id=1, source_target_pairs={{0,8},{8,16},{16,24},{24,0},{1,9},{9,17},{17,25},{25,1},{2,10},{10... | collective-permute-start | bytes 786440 | tf_op jit(solution)/shard_map/ppermute | solution.py:407
  154.9 43.4 %collective-permute-start.24 = (bf16[256,1024]{1,0:T(8,128)(2,1)}, bf16[256,1024]{1,0:T(8,128)(2,1)S(1)}, u32[]{:S(2)}, u32[]{:S(2)}) collective-permute-start(bf16[256,1024]{1,0:T(8,128)(2,1)} %get-tuple-element.36), channel_id=1, source_target_pairs={{0,2},{8,10},{16,18},{24,26},{32,34},{40,42},{48,50},{56,58},{64,6... | collective-permute-start | bytes 1572872 | tf_op jit(solution)/shard_map/ppermute | solution.py:400
  158.8 39.5 %collective-permute-start.25 = (bf16[256,1024]{1,0:T(8,128)(2,1)}, bf16[256,1024]{1,0:T(8,128)(2,1)}, u32[]{:S(2)}, u32[]{:S(2)}) collective-permute-start(bf16[256,1024]{1,0:T(8,128)(2,1)} %get-tuple-element.37), channel_id=1, source_target_pairs={{0,4},{8,12},{16,20},{24,28},{32,36},{40,44},{48,52},{56,60},{64,6... | collective-permute-start | bytes 1572872 | tf_op jit(solution)/shard_map/ppermute | solution.py:400
  161.8 36.5 %collective-permute-start.26 = (bf16[256,1024]{1,0:T(8,128)(2,1)}, bf16[256,1024]{1,0:T(8,128)(2,1)}, u32[]{:S(2)}, u32[]{:S(2)}) collective-permute-start(bf16[256,1024]{1,0:T(8,128)(2,1)} %get-tuple-element.38), channel_id=1, source_target_pairs={{0,6},{8,14},{16,22},{24,30},{32,38},{40,46},{48,54},{56,62},{64,7... | collective-permute-start | bytes 1572872 | tf_op jit(solution)/shard_map/ppermute | solution.py:400
  195.5 10.4 %collective-permute-start.28 = (bf16[1024,256]{1,0:T(8,128)(2,1)}, bf16[1024,256]{1,0:T(8,128)(2,1)S(1)}, u32[]{:S(2)}, u32[]{:S(2)}) collective-permute-start(bf16[1024,256]{1,0:T(8,128)(2,1)} %get-tuple-element.39), channel_id=1, source_target_pairs={{0,8},{1,9},{2,10},{3,11},{4,12},{5,13},{6,14},{7,15},{32,40},{33,... | collective-permute-start | bytes 1572872 | tf_op jit(solution)/shard_map/ppermute | solution.py:471
  197.0 10.3 %collective-permute-start.29 = (bf16[1024,256]{1,0:T(8,128)(2,1)}, bf16[1024,256]{1,0:T(8,128)(2,1)S(1)}, u32[]{:S(2)}, u32[]{:S(2)}) collective-permute-start(bf16[1024,256]{1,0:T(8,128)(2,1)} %get-tuple-element.40), channel_id=1, source_target_pairs={{0,24},{1,25},{2,26},{3,27},{4,28},{5,29},{6,30},{7,31},{32,56},{3... | collective-permute-start | bytes 1572872 | tf_op jit(solution)/shard_map/ppermute | solution.py:474
  198.6 18.2 %collective-permute-start.27 = (bf16[128,1024]{1,0:T(8,128)(2,1)S(1)}, bf16[128,1024]{1,0:T(8,128)(2,1)S(1)}, u32[]{:S(2)}, u32[]{:S(2)}) collective-permute-start(bf16[128,1024]{1,0:T(8,128)(2,1)S(1)} %slice.23), channel_id=1, source_target_pairs={{0,1},{2,3},{4,5},{6,7},{8,9},{10,11},{12,13},{14,15},{16,17},{18,... | collective-permute-start | bytes 786440 | tf_op jit(solution)/shard_map/ppermute | solution.py:402
  209.1 17.7 %collective-permute-start.30 = (bf16[1024,256]{1,0:T(8,128)(2,1)}, bf16[1024,256]{1,0:T(8,128)(2,1)}, u32[]{:S(2)}, u32[]{:S(2)}) collective-permute-start(bf16[1024,256]{1,0:T(8,128)(2,1)} %broadcast_select_fusion.3), channel_id=1, source_target_pairs={{0,8},{8,16},{1,9},{9,17},{2,10},{10,18},{3,11},{11,19},{4,12},{12... | collective-permute-start | bytes 1572872 | tf_op jit(solution)/shard_map/ppermute | solution.py:471
  212.8 14.0 %collective-permute-start.31 = (bf16[1024,256]{1,0:T(8,128)(2,1)}, bf16[1024,256]{1,0:T(8,128)(2,1)}, u32[]{:S(2)}, u32[]{:S(2)}) collective-permute-start(bf16[1024,256]{1,0:T(8,128)(2,1)} %broadcast_select_fusion.2), channel_id=1, source_target_pairs={{0,24},{24,16},{1,25},{25,17},{2,26},{26,18},{3,27},{27,19},{4,28}... | collective-permute-start | bytes 1572872 | tf_op jit(solution)/shard_map/ppermute | solution.py:474
  222.2 30.6 %all-to-all-start.4 = ((bf16[8,128,1024]{2,1,0:T(8,128)(2,1)}), bf16[8,128,1024]{2,1,0:T(8,128)(2,1)S(1)}, u32[]{:S(2)}, u32[]{:S(2)}) async-start(bf16[8,128,1024]{2,1,0:T(8,128)(2,1)} %shard_map.74), calls=%async_computation.4 | async-start | bytes 4194304 | tf_op jit(solution)/shard_map/all_to_all | solution.py:468
  228.0 10.4 %collective-permute-start.32 = (bf16[1024,256]{1,0:T(8,128)(2,1)}, bf16[1024,256]{1,0:T(8,128)(2,1)}, u32[]{:S(2)}, u32[]{:S(2)}) collective-permute-start(bf16[1024,256]{1,0:T(8,128)(2,1)} %get-tuple-element.49), channel_id=1, source_target_pairs={{0,8},{8,16},{16,24},{1,9},{9,17},{17,25},{2,10},{10,18},{18,26},{... | collective-permute-start | bytes 1572872 | tf_op jit(solution)/shard_map/ppermute | solution.py:471
  230.1 10.7 %collective-permute-start.33 = (bf16[1024,256]{1,0:T(8,128)(2,1)}, bf16[1024,256]{1,0:T(8,128)(2,1)}, u32[]{:S(2)}, u32[]{:S(2)}) collective-permute-start(bf16[1024,256]{1,0:T(8,128)(2,1)} %get-tuple-element.50), channel_id=1, source_target_pairs={{0,24},{24,16},{16,8},{1,25},{25,17},{17,9},{2,26},{26,18},{18,10}... | collective-permute-start | bytes 1572872 | tf_op jit(solution)/shard_map/ppermute | solution.py:474
  234.2 10.1 %collective-permute-start.36 = (bf16[256,256]{1,0:T(8,128)(2,1)S(1)}, bf16[256,256]{1,0:T(8,128)(2,1)S(1)}, u32[]{:S(2)}, u32[]{:S(2)}) collective-permute-start(bf16[256,256]{1,0:T(8,128)(2,1)S(1)} %copy-done.13), channel_id=1, source_target_pairs={{8,0},{9,1},{18,10},{19,11},{28,20},{29,21},{6,30},{7,31},{40,32},... | collective-permute-start | bytes 393224 | tf_op jit(solution)/shard_map/ppermute | solution.py:465
  (53 other events, 359.5 us)
